TPU v7x, 512 devices: a whole 4x8x8 slice. The times are simulated.
512 devices in a mesh: ka: 32 (over x_lo, y, core), pb: 16 (over x_hi, z).
Axes of the slice: x: 4 (x_hi: 2, x_lo: 2; x = x_hi * 2 + x_lo), y: 8, z: 8, core: 2. Of those that a mesh axis runs over, the one named last changes fastest.
Arguments:
- targets: bfloat16 [32, 4, 2, 32768], P('ka'), may hold values from -6 to 6
- partners: bfloat16 [16, 2, 2, 32768], P('pb', None, None, 'ka'), may hold values from -6 to 6
- pair_map: int32 [32, 16], P('ka', 'pb'), may hold values from 0 to 63
- shifts: int32 [32, 16, 3], P('ka', 'pb'), may hold values from 0 to 1
Outputs:
- projector: float32 [32, 8, 2, 32768], P('ka', None, None, 'pb')
Inputs may be any that keep to these rules, and one draw needn't show every extreme that they name: d = pair_map[k,q] names the mesh point (d // 16, (d // 4) mod 4, d mod 4).
All inputs are finite; a program needn't handle non-finite values.
Results may differ from a plain program's by a relative error of at most 0.015.
Values may be sent and summed in bfloat16 or wider, within the bound.
No kernel may reach another device: no remote copies, remote signals or barrier semaphores. Data moves between devices by JAX's collectives and lax.ppermute only.
A program may use at most 64 MiB of HBM per device.

v0:
```python
import jax
import jax.numpy as jnp
from jax import lax
from jax.sharding import PartitionSpec as P

GRID = 32


KPOINT_SCALING = 2.0
SCREENING_CUTOFF = 0.25
FORMS = ("anbm,pbxym->paxyn", "anbm,pbxmz->paxnz", "anbm,pbmyz->panyz")


def copy_for_each(array, axis):
    length = lax.axis_size(axis)
    return lax.all_to_all(
        jnp.broadcast_to(array[None], (length, *array.shape)), axis, 0, 0, tiled=True
    )


def laid_out(tiles, dim):
    tiles = jnp.moveaxis(tiles, 0, dim)
    lengths = tiles.shape
    return tiles.reshape(*lengths[:dim], lengths[dim] * lengths[dim + 1], *lengths[dim + 2 :])


def gathered_copies(array, axis, dim):
    tiles = copy_for_each(array, axis)
    return laid_out(tiles, dim)


def split_up(array, dim, length):
    lengths = array.shape
    tiles = array.reshape(*lengths[:dim], length, lengths[dim] // length, *lengths[dim + 1 :])
    return jnp.moveaxis(tiles, dim, 0)


def sum_at_owner(array, axis, dim):
    tiles = split_up(array, dim, lax.axis_size(axis))
    arrived = lax.all_to_all(tiles, axis, split_axis=0, concat_axis=0, tiled=True)
    return arrived.astype(jnp.float32).sum(axis=0)


def taken_together(array, axis):
    return copy_for_each(array, axis).sum(axis=0)


def dft_tables(length):
    counter = jnp.arange(length, dtype=jnp.int32)
    product = counter[:, None] * counter[None, :] % length
    angles = product.astype(jnp.float32) * (2.0 * jnp.pi / length)
    cos_table = jnp.cos(angles)
    sine_lookup_table = jnp.sin(angles)
    forward = jnp.stack(
        [
            jnp.stack([cos_table, sine_lookup_table], 1),
            jnp.stack([-sine_lookup_table, cos_table], 1),
        ],
        0,
    )
    inverse = jnp.stack(
        [
            jnp.stack([cos_table, -sine_lookup_table], 1),
            jnp.stack([sine_lookup_table, cos_table], 1),
        ],
        0,
    )
    return (forward.astype(jnp.bfloat16), inverse.astype(jnp.bfloat16))


def coulomb(offset, shift, length):
    counter = jnp.arange(length, dtype=jnp.int32)
    frequency = ((counter + length // 2) % length - length // 2).astype(jnp.float32)
    lattice = (offset // 16, offset // 4 % 4, offset % 4)
    components = [
        frequency + shift[axis_id].astype(jnp.float32) + lattice[axis_id].astype(jnp.float32) * 0.25
        for axis_id in range(3)
    ]
    squared_magnitude = (
        (components[0] * components[0])[:, None, None]
        + (components[1] * components[1])[None, :, None]
        + (components[2] * components[2])[None, None, :]
    )
    return KPOINT_SCALING / (squared_magnitude + SCREENING_CUTOFF)


def transform(exchange_matrix, blocks, form):
    return jnp.einsum(form, exchange_matrix, blocks, preferred_element_type=jnp.float32)


def band_field(target, partners, kernel, forward, inverse, length):
    cells = length**3
    part_re = partners[:, 0].astype(jnp.float32)
    part_im = partners[:, 1].astype(jnp.float32)
    targ_re = target[0].astype(jnp.float32)
    targ_im = target[1].astype(jnp.float32)
    density = jnp.stack(
        [part_re * targ_re + part_im * targ_im, part_re * targ_im - part_im * targ_re], 1
    )
    blocks = density.astype(jnp.bfloat16).reshape(-1, 2, length, length, length)
    blocks = transform(forward, blocks, FORMS[0]).astype(jnp.bfloat16)
    blocks = transform(forward, blocks, FORMS[1]).astype(jnp.bfloat16)
    spectrum = transform(forward, blocks, FORMS[2])
    blocks = (spectrum * kernel).astype(jnp.bfloat16)
    blocks = transform(inverse, blocks, FORMS[2]).astype(jnp.bfloat16)
    blocks = transform(inverse, blocks, FORMS[1]).astype(jnp.bfloat16)
    potential = transform(inverse, blocks, FORMS[0]).reshape(-1, 2, cells) * (1.0 / cells)
    pot_re = potential[:, 0]
    pot_im = potential[:, 1]
    return -jnp.stack(
        [
            jnp.sum(part_re * pot_re - part_im * pot_im, 0),
            jnp.sum(part_re * pot_im + part_im * pot_re, 0),
        ],
        0,
    )


def real_vectors(fields):
    real_part = fields[:, 0]
    imag_part = fields[:, 1]
    return jnp.concatenate(
        [jnp.concatenate([real_part, imag_part], 1), jnp.concatenate([-imag_part, real_part], 1)], 0
    )


def partial_intersection(target_set, fields):
    basis_set = real_vectors(target_set.astype(jnp.float32))
    return jnp.dot(basis_set, real_vectors(fields).T, precision=lax.Precision.HIGHEST)


def local(targets, partners, pair_map, shifts):
    length = GRID
    cells = length**3
    forward, inverse = dft_tables(length)
    target_set = targets[0]
    occupied_orbitals = gathered_copies(partners[0], "ka", 2)
    kernel = coulomb(pair_map[0, 0], shifts[0, 0], length)
    share_cells = cells // lax.axis_size("pb")
    start = lax.axis_index("pb") * share_cells

    def one_share(carry, orbital):
        fields = band_field(orbital, occupied_orbitals, kernel, forward, inverse, length)
        return (carry, sum_at_owner(fields.astype(jnp.bfloat16), "pb", 1))

    unused, own_fields = lax.scan(one_share, jnp.zeros((), jnp.float32), target_set)
    own_targets = lax.dynamic_slice_in_dim(target_set, start, share_cells, 2)
    intersection = taken_together(partial_intersection(own_targets, own_fields), "pb")
    intersection = intersection * (1.0 / cells)
    exchange_matrix = -0.5 * (intersection + intersection.T)
    prefactor_value = jnp.linalg.cholesky(exchange_matrix)
    images = real_vectors(own_fields)
    solved = lax.linalg.triangular_solve(prefactor_value, images, left_side=True, lower=True)
    return solved.reshape(images.shape[0], 2, share_cells)[None]


def solution(mesh):
    return jax.shard_map(
        local,
        mesh=mesh,
        in_specs=(
            P("ka", None, None, None),
            P("pb", None, None, "ka"),
            P("ka", "pb"),
            P("ka", "pb", None),
        ),
        out_specs=P("ka", None, None, "pb"),
        check_vma=False,
    )
```

profile of v0, /device:TPU:8, one launch (start us, length us, event | category | flops | bytes accessed | tf_op | source)
XLA Modules:
  0.0 181.2 jit_solution(6275062098875357921)
XLA Ops:
  7.5 9.3 %all-to-all-start.1 = ((bf16[32,2,2,1024]{3,2,1,0:T(2,128)(2,1)}), bf16[32,2,2,1024]{3,2,1,0:T(2,128)(2,1)S(1)}, u32[]{:S(2)}, u32[]{:S(2)}) async-start(bf16[32,2,2,1024]{3,2,1,0:T(2,128)(2,1)} %broadcast_in_dim.14), calls=%async_computation.1 | async-start | bytes 524288 | tf_op jit(solution)/shard_map/all_to_all | solution.py:16
  17.5 11.5 %all-to-all-done.1 = bf16[32,2,2,1024]{3,2,1,0:T(2,128)(2,1)S(1)} async-done(((bf16[32,2,2,1024]{3,2,1,0:T(2,128)(2,1)}), bf16[32,2,2,1024]{3,2,1,0:T(2,128)(2,1)S(1)}, u32[]{:S(2)}, u32[]{:S(2)}) %all-to-all-start.1) | async-done | bytes 262176 | tf_op jit(solution)/shard_map/all_to_all | solution.py:16
  29.2 132.6 %while.11 = (s32[]{:T(128)}, f32[4,2,2048]{2,1,0:T(2,128)S(1)}, bf16[2,2,32768]{2,1,0:T(2,128)(2,1)S(1)}, bf16[4,2,32768]{2,1,0:T(2,128)(2,1)}, bf16[2,32,2,32]{...) while((s32[]{:T(128)}, f32[4,2,2048]{2,1,0:T(2,128)S(1)}, ...), condition=%wide.region_4.5_spmd.clone, body=%wide.region_0.4_spmd.clone.sunk | while | flops 103837696 | bytes 9000293 | solution.py:146
  30.4 2.1 %convert_reduce_fusion.5 = (bf16[2,32768]{1,0:T(2,128)(2,1)S(1)}, bf16[2,32768]{1,0:T(2,128)(2,1)S(1)}) fusion(f32[32768]{0:T(1024)S(1)} %bitcast.230, f32[32768]{0:T(1024)S(1)} %bitcast.229, bf16[2,2,32768]{2,1,0:T(2,128)(2,1)S(1)} %get-tuple-element.203), kind=kLoop, calls=%fused_computation.24.clone.1 | loop fusion | flops 655360 | bytes 786432 | tf_op jit(solution)/shard_map/convert.5
  34.0 2.2 %copy.108 = bf16[2,2,32,32,32,1]{2,4,1,5,3,0:T(8,128)(2,1)S(1)} copy(bf16[2,2,32,32,32,1]{3,4,1,2,0,5:T(8,128)(2,1)S(1)} %fusion.77) | data formatting | bytes 524288 | tf_op jit(solution)/shard_map/while/body/eval_jaxpr/convert_element_type | solution.py:102
  37.2 2.2 %copy.109 = bf16[2,2,32,32,32,1]{3,4,1,5,2,0:T(8,128)(2,1)S(1)} copy(bf16[2,2,32,32,32,1]{2,4,1,3,0,5:T(8,128)(2,1)S(1)} %fusion.78) | data formatting | bytes 524288 | tf_op jit(solution)/shard_map/while/body/eval_jaxpr/convert_element_type | solution.py:105
  40.3 1.6 copy.110
  41.9 2.3 %mul.380 = f32[2,2,32768]{2,1,0:T(2,128)S(1)} reshape(f32[2,2,32,32,32]{4,3,2,1,0:T(8,128)} %copy.110) | data formatting | bytes 1048576 | tf_op jit(solution)/shard_map/while/body/eval_jaxpr/mul | solution.py:107
  46.6 11.8 %all-to-all-start = ((bf16[16,2,2048]{2,1,0:T(2,128)(2,1)}), bf16[16,2,2048]{2,1,0:T(2,128)(2,1)S(1)}, u32[]{:S(2)}, u32[]{:S(2)}) async-start(bf16[16,2,2048]{2,1,0:T(2,128)(2,1)} %fusion.80), calls=%async_computation | async-start | bytes 262144 | tf_op jit(solution)/shard_map/while/body/eval_jaxpr/all_to_all | solution.py:40
  58.4 10.1 %all-to-all-done = bf16[16,2,2048]{2,1,0:T(2,128)(2,1)S(1)} async-done(((bf16[16,2,2048]{2,1,0:T(2,128)(2,1)}), bf16[16,2,2048]{2,1,0:T(2,128)(2,1)S(1)}, u32[]{:S(2)}, u32[]{:S(2)}) %all-to-all-start) | async-done | bytes 131104 | tf_op jit(solution)/shard_map/while/body/eval_jaxpr/all_to_all | solution.py:40
  69.8 2.1 %convert_reduce_fusion.5 = (bf16[2,32768]{1,0:T(2,128)(2,1)S(1)}, bf16[2,32768]{1,0:T(2,128)(2,1)S(1)}) fusion(f32[32768]{0:T(1024)S(1)} %bitcast.230, f32[32768]{0:T(1024)S(1)} %bitcast.229, bf16[2,2,32768]{2,1,0:T(2,128)(2,1)S(1)} %get-tuple-element.203), kind=kLoop, calls=%fused_computation.24.clone.1 | loop fusion | flops 655360 | bytes 786432 | tf_op jit(solution)/shard_map/convert.5
  73.4 2.2 %copy.108 = bf16[2,2,32,32,32,1]{2,4,1,5,3,0:T(8,128)(2,1)S(1)} copy(bf16[2,2,32,32,32,1]{3,4,1,2,0,5:T(8,128)(2,1)S(1)} %fusion.77) | data formatting | bytes 524288 | tf_op jit(solution)/shard_map/while/body/eval_jaxpr/convert_element_type | solution.py:102
  76.6 2.2 %copy.109 = bf16[2,2,32,32,32,1]{3,4,1,5,2,0:T(8,128)(2,1)S(1)} copy(bf16[2,2,32,32,32,1]{2,4,1,3,0,5:T(8,128)(2,1)S(1)} %fusion.78) | data formatting | bytes 524288 | tf_op jit(solution)/shard_map/while/body/eval_jaxpr/convert_element_type | solution.py:105
  79.7 1.6 copy.110
  81.2 2.3 %mul.380 = f32[2,2,32768]{2,1,0:T(2,128)S(1)} reshape(f32[2,2,32,32,32]{4,3,2,1,0:T(8,128)} %copy.110) | data formatting | bytes 1048576 | tf_op jit(solution)/shard_map/while/body/eval_jaxpr/mul | solution.py:107
  86.0 3.5 %all-to-all-start = ((bf16[16,2,2048]{2,1,0:T(2,128)(2,1)}), bf16[16,2,2048]{2,1,0:T(2,128)(2,1)S(1)}, u32[]{:S(2)}, u32[]{:S(2)}) async-start(bf16[16,2,2048]{2,1,0:T(2,128)(2,1)} %fusion.80), calls=%async_computation | async-start | bytes 262144 | tf_op jit(solution)/shard_map/while/body/eval_jaxpr/all_to_all | solution.py:40
  89.5 10.0 %all-to-all-done = bf16[16,2,2048]{2,1,0:T(2,128)(2,1)S(1)} async-done(((bf16[16,2,2048]{2,1,0:T(2,128)(2,1)}), bf16[16,2,2048]{2,1,0:T(2,128)(2,1)S(1)}, u32[]{:S(2)}, u32[]{:S(2)}) %all-to-all-start) | async-done | bytes 131104 | tf_op jit(solution)/shard_map/while/body/eval_jaxpr/all_to_all | solution.py:40
  100.9 2.1 %convert_reduce_fusion.5 = (bf16[2,32768]{1,0:T(2,128)(2,1)S(1)}, bf16[2,32768]{1,0:T(2,128)(2,1)S(1)}) fusion(f32[32768]{0:T(1024)S(1)} %bitcast.230, f32[32768]{0:T(1024)S(1)} %bitcast.229, bf16[2,2,32768]{2,1,0:T(2,128)(2,1)S(1)} %get-tuple-element.203), kind=kLoop, calls=%fused_computation.24.clone.1 | loop fusion | flops 655360 | bytes 786432 | tf_op jit(solution)/shard_map/convert.5
  104.4 2.2 %copy.108 = bf16[2,2,32,32,32,1]{2,4,1,5,3,0:T(8,128)(2,1)S(1)} copy(bf16[2,2,32,32,32,1]{3,4,1,2,0,5:T(8,128)(2,1)S(1)} %fusion.77) | data formatting | bytes 524288 | tf_op jit(solution)/shard_map/while/body/eval_jaxpr/convert_element_type | solution.py:102
  107.6 2.2 %copy.109 = bf16[2,2,32,32,32,1]{3,4,1,5,2,0:T(8,128)(2,1)S(1)} copy(bf16[2,2,32,32,32,1]{2,4,1,3,0,5:T(8,128)(2,1)S(1)} %fusion.78) | data formatting | bytes 524288 | tf_op jit(solution)/shard_map/while/body/eval_jaxpr/convert_element_type | solution.py:105
  110.7 1.6 copy.110
  112.3 2.3 %mul.380 = f32[2,2,32768]{2,1,0:T(2,128)S(1)} reshape(f32[2,2,32,32,32]{4,3,2,1,0:T(8,128)} %copy.110) | data formatting | bytes 1048576 | tf_op jit(solution)/shard_map/while/body/eval_jaxpr/mul | solution.py:107
  117.0 3.5 %all-to-all-start = ((bf16[16,2,2048]{2,1,0:T(2,128)(2,1)}), bf16[16,2,2048]{2,1,0:T(2,128)(2,1)S(1)}, u32[]{:S(2)}, u32[]{:S(2)}) async-start(bf16[16,2,2048]{2,1,0:T(2,128)(2,1)} %fusion.80), calls=%async_computation | async-start | bytes 262144 | tf_op jit(solution)/shard_map/while/body/eval_jaxpr/all_to_all | solution.py:40
  120.5 10.0 %all-to-all-done = bf16[16,2,2048]{2,1,0:T(2,128)(2,1)S(1)} async-done(((bf16[16,2,2048]{2,1,0:T(2,128)(2,1)}), bf16[16,2,2048]{2,1,0:T(2,128)(2,1)S(1)}, u32[]{:S(2)}, u32[]{:S(2)}) %all-to-all-start) | async-done | bytes 131104 | tf_op jit(solution)/shard_map/while/body/eval_jaxpr/all_to_all | solution.py:40
  131.9 2.1 %convert_reduce_fusion.5 = (bf16[2,32768]{1,0:T(2,128)(2,1)S(1)}, bf16[2,32768]{1,0:T(2,128)(2,1)S(1)}) fusion(f32[32768]{0:T(1024)S(1)} %bitcast.230, f32[32768]{0:T(1024)S(1)} %bitcast.229, bf16[2,2,32768]{2,1,0:T(2,128)(2,1)S(1)} %get-tuple-element.203), kind=kLoop, calls=%fused_computation.24.clone.1 | loop fusion | flops 655360 | bytes 786432 | tf_op jit(solution)/shard_map/convert.5
  135.5 2.2 %copy.108 = bf16[2,2,32,32,32,1]{2,4,1,5,3,0:T(8,128)(2,1)S(1)} copy(bf16[2,2,32,32,32,1]{3,4,1,2,0,5:T(8,128)(2,1)S(1)} %fusion.77) | data formatting | bytes 524288 | tf_op jit(solution)/shard_map/while/body/eval_jaxpr/convert_element_type | solution.py:102
  138.7 2.2 %copy.109 = bf16[2,2,32,32,32,1]{3,4,1,5,2,0:T(8,128)(2,1)S(1)} copy(bf16[2,2,32,32,32,1]{2,4,1,3,0,5:T(8,128)(2,1)S(1)} %fusion.78) | data formatting | bytes 524288 | tf_op jit(solution)/shard_map/while/body/eval_jaxpr/convert_element_type | solution.py:105
  143.4 2.3 %mul.380 = f32[2,2,32768]{2,1,0:T(2,128)S(1)} reshape(f32[2,2,32,32,32]{4,3,2,1,0:T(8,128)} %copy.110) | data formatting | bytes 1048576 | tf_op jit(solution)/shard_map/while/body/eval_jaxpr/mul | solution.py:107
  148.1 3.5 %all-to-all-start = ((bf16[16,2,2048]{2,1,0:T(2,128)(2,1)}), bf16[16,2,2048]{2,1,0:T(2,128)(2,1)S(1)}, u32[]{:S(2)}, u32[]{:S(2)}) async-start(bf16[16,2,2048]{2,1,0:T(2,128)(2,1)} %fusion.80), calls=%async_computation | async-start | bytes 262144 | tf_op jit(solution)/shard_map/while/body/eval_jaxpr/all_to_all | solution.py:40
  151.6 10.0 %all-to-all-done = bf16[16,2,2048]{2,1,0:T(2,128)(2,1)S(1)} async-done(((bf16[16,2,2048]{2,1,0:T(2,128)(2,1)}), bf16[16,2,2048]{2,1,0:T(2,128)(2,1)S(1)}, u32[]{:S(2)}, u32[]{:S(2)}) %all-to-all-start) | async-done | bytes 131104 | tf_op jit(solution)/shard_map/while/body/eval_jaxpr/all_to_all | solution.py:40
  163.8 3.5 %all-to-all-start.2 = ((f32[16,8,8]{2,1,0:T(8,128)}), f32[16,8,8]{2,1,0:T(8,128)S(1)}, u32[]{:S(2)}, u32[]{:S(2)}) async-start(f32[16,8,8]{2,1,0:T(8,128)} %broadcast_in_dim.21), calls=%async_computation.2 | async-start | bytes 131072 | tf_op jit(solution)/shard_map/all_to_all | solution.py:16
  167.3 10.0 %all-to-all-done.2 = f32[16,8,8]{2,1,0:T(8,128)S(1)} async-done(((f32[16,8,8]{2,1,0:T(8,128)}), f32[16,8,8]{2,1,0:T(8,128)S(1)}, u32[]{:S(2)}, u32[]{:S(2)}) %all-to-all-start.2) | async-done | bytes 4128 | tf_op jit(solution)/shard_map/all_to_all | solution.py:16
  (95 shorter events, 40.8 us)
Async XLA Ops:
  7.5 21.5 %all-to-all-start.1 = ((bf16[32,2,2,1024]{3,2,1,0:T(2,128)(2,1)}), bf16[32,2,2,1024]{3,2,1,0:T(2,128)(2,1)S(1)}, u32[]{:S(2)}, u32[]{:S(2)}) async-start(bf16[32,2,2,1024]{3,2,1,0:T(2,128)(2,1)} %broadcast_in_dim.14), calls=%async_computation.1 | async-start | bytes 524288 | tf_op jit(solution)/shard_map/all_to_all | solution.py:16
  29.2 7.0 %copy-start = (f32[32]{0:T(128)}, f32[32]{0:T(128)S(1)}, u32[]{:S(2)}) copy-start(f32[32]{0:T(128)S(1)} %get-tuple-element.207) | copy-start | bytes 388 | tf_op jit(solution)/shard_map/while
  41.8 26.7 %copy-start.1 = (f32[32]{0:T(128)S(1)}, f32[32]{0:T(128)}, u32[]{:S(2)}) copy-start(f32[32]{0:T(128)} %copy-done) | copy-start | bytes 388 | tf_op jit(solution)/shard_map/while
  46.6 21.9 %all-to-all-start = ((bf16[16,2,2048]{2,1,0:T(2,128)(2,1)}), bf16[16,2,2048]{2,1,0:T(2,128)(2,1)S(1)}, u32[]{:S(2)}, u32[]{:S(2)}) async-start(bf16[16,2,2048]{2,1,0:T(2,128)(2,1)} %fusion.80), calls=%async_computation | async-start | bytes 262144 | tf_op jit(solution)/shard_map/while/body/eval_jaxpr/all_to_all | solution.py:40
  68.6 7.0 %copy-start = (f32[32]{0:T(128)}, f32[32]{0:T(128)S(1)}, u32[]{:S(2)}) copy-start(f32[32]{0:T(128)S(1)} %get-tuple-element.207) | copy-start | bytes 388 | tf_op jit(solution)/shard_map/while
  81.2 18.4 %copy-start.1 = (f32[32]{0:T(128)S(1)}, f32[32]{0:T(128)}, u32[]{:S(2)}) copy-start(f32[32]{0:T(128)} %copy-done) | copy-start | bytes 388 | tf_op jit(solution)/shard_map/while
  86.0 13.6 %all-to-all-start = ((bf16[16,2,2048]{2,1,0:T(2,128)(2,1)}), bf16[16,2,2048]{2,1,0:T(2,128)(2,1)S(1)}, u32[]{:S(2)}, u32[]{:S(2)}) async-start(bf16[16,2,2048]{2,1,0:T(2,128)(2,1)} %fusion.80), calls=%async_computation | async-start | bytes 262144 | tf_op jit(solution)/shard_map/while/body/eval_jaxpr/all_to_all | solution.py:40
  99.7 7.0 %copy-start = (f32[32]{0:T(128)}, f32[32]{0:T(128)S(1)}, u32[]{:S(2)}) copy-start(f32[32]{0:T(128)S(1)} %get-tuple-element.207) | copy-start | bytes 388 | tf_op jit(solution)/shard_map/while
  112.3 18.4 %copy-start.1 = (f32[32]{0:T(128)S(1)}, f32[32]{0:T(128)}, u32[]{:S(2)}) copy-start(f32[32]{0:T(128)} %copy-done) | copy-start | bytes 388 | tf_op jit(solution)/shard_map/while
  117.0 13.6 %all-to-all-start = ((bf16[16,2,2048]{2,1,0:T(2,128)(2,1)}), bf16[16,2,2048]{2,1,0:T(2,128)(2,1)S(1)}, u32[]{:S(2)}, u32[]{:S(2)}) async-start(bf16[16,2,2048]{2,1,0:T(2,128)(2,1)} %fusion.80), calls=%async_computation | async-start | bytes 262144 | tf_op jit(solution)/shard_map/while/body/eval_jaxpr/all_to_all | solution.py:40
  130.7 7.0 %copy-start = (f32[32]{0:T(128)}, f32[32]{0:T(128)S(1)}, u32[]{:S(2)}) copy-start(f32[32]{0:T(128)S(1)} %get-tuple-element.207) | copy-start | bytes 388 | tf_op jit(solution)/shard_map/while
  143.4 18.4 %copy-start.1 = (f32[32]{0:T(128)S(1)}, f32[32]{0:T(128)}, u32[]{:S(2)}) copy-start(f32[32]{0:T(128)} %copy-done) | copy-start | bytes 388 | tf_op jit(solution)/shard_map/while
  148.1 13.6 %all-to-all-start = ((bf16[16,2,2048]{2,1,0:T(2,128)(2,1)}), bf16[16,2,2048]{2,1,0:T(2,128)(2,1)S(1)}, u32[]{:S(2)}, u32[]{:S(2)}) async-start(bf16[16,2,2048]{2,1,0:T(2,128)(2,1)} %fusion.80), calls=%async_computation | async-start | bytes 262144 | tf_op jit(solution)/shard_map/while/body/eval_jaxpr/all_to_all | solution.py:40
  163.8 13.5 %all-to-all-start.2 = ((f32[16,8,8]{2,1,0:T(8,128)}), f32[16,8,8]{2,1,0:T(8,128)S(1)}, u32[]{:S(2)}, u32[]{:S(2)}) async-start(f32[16,8,8]{2,1,0:T(8,128)} %broadcast_in_dim.21), calls=%async_computation.2 | async-start | bytes 131072 | tf_op jit(solution)/shard_map/all_to_all | solution.py:16
where the time goes:
time: 182 us; the launch traced here: 181 us
  waiting for transfers between devices  61.7 us (34%)
  local copies, waits for them, and re-layouts  40.9 us (22%)
  starting transfers between devices  35.1 us (19%)
  other arithmetic  28.3 us (16%)
  matrix products  11.8 us (6%)
  between operations  2.81 us (2%)
    all_to_all x4, waiting for transfers between devices, sum_at_owner(): lax.all_to_all(tiles, axis, split_axis=0, concat_axis=0, tiled=True)  40.2 us
    all_to_all x4, starting transfers between devices, sum_at_owner(): lax.all_to_all(tiles, axis, split_axis=0, concat_axis=0, tiled=True)  22.3 us
    all_to_all x2, waiting for transfers between devices, copy_for_each(): lax.all_to_all(jnp.broadcast_to(array[None], (length, *array.shape)), axi...  21.5 us
    mul x8, local copies, waits for them, and re-layouts, band_field(): transform(inverse, blocks, FORMS[0]).reshape(-1, 2, cells) * (1.0 / cells)  15.6 us
    all_to_all x2, starting transfers between devices, copy_for_each(): lax.all_to_all(jnp.broadcast_to(array[None], (length, *array.shape)), axi...  12.8 us
    dot_general x12, matrix products, transform(): jnp.einsum(form, exchange_matrix, blocks, preferred_element_type=jnp.floa...  10.3 us
    convert_element_type x4, local copies, waits for them, and re-layouts, band_field(): blocks = transform(inverse, blocks, FORMS[2]).astype(jnp.bfloat16)  8.86 us
    convert_element_type x4, local copies, waits for them, and re-layouts, band_field(): blocks = transform(forward, blocks, FORMS[1]).astype(jnp.bfloat16)  8.86 us
  transfers between devices with their start and end apart: 6, of which 6 were waited for; matrix products, arithmetic and copies ran while one was open for 0% of the time, Pallas kernels for 0%

commit v1 on v0

v1 whole, which is shorter than its diff:
```python
import jax
import jax.numpy as jnp
import numpy as np
from jax import lax
from jax.experimental import pallas as pl
from jax.experimental.pallas import tpu as pltpu
from jax.sharding import PartitionSpec as P

GRID = 32
BANDS = 4
OCC = 2
PLANE = 8
ROWS = GRID * PLANE
CELLS = GRID**3
KPOINT_SCALING = 2.0
SCREENING_CUTOFF = 0.25
PAIRS = [(i, j) for i in range(BANDS) for j in range(i, BANDS)]
EXTRA = 8


def phases(angle):
    turn = 2.0 * np.pi * (angle % GRID) / GRID
    return np.cos(turn), np.sin(turn)


def tables():
    row = np.arange(ROWS)
    lane = np.arange(128)
    hi, lo = row // PLANE, row % PLANE
    cos, sin = phases(hi[:, None] * hi[None] + 4 * lo[:, None] * lo[None])
    left = np.block([[cos, sin], [-sin, cos]])
    part, z = lane // GRID, lane % GRID
    cos, sin = phases(z[:, None] * z[None] + 8 * part[:, None] * part[None])
    right = np.block([[cos, -sin], [sin, cos]])
    twist = np.stack(phases(lo[:, None] * part[None]))
    return left.astype(jnp.bfloat16), right.astype(jnp.bfloat16), twist.astype(np.float32)


def wave_number(index):
    return ((index + GRID // 2) % GRID - GRID // 2).astype(jnp.float32)


def coulomb(offset, shift):
    row = lax.broadcasted_iota(jnp.int32, (ROWS, 128), 0)
    lane = lax.broadcasted_iota(jnp.int32, (ROWS, 128), 1)
    index = (row // PLANE, (lane // GRID) * PLANE + row % PLANE, lane % GRID)
    lattice = (offset // 16, offset // 4 % 4, offset % 4)
    squared = jnp.zeros((ROWS, 128), jnp.float32)
    for axis in range(3):
        moved = shift[axis].astype(jnp.float32) + lattice[axis].astype(jnp.float32) * 0.25
        component = wave_number(index[axis]) + moved
        squared += component * component
    return KPOINT_SCALING / (squared + SCREENING_CUTOFF)


def product(a, b):
    return jnp.dot(a, b, preferred_element_type=jnp.float32)


def exchange_kernel(offset, shift, targets, partners, left, right, twist, out, kernel):
    kernel[...] = coulomb(offset[0, 0], [shift[0, 0, axis] for axis in range(3)]) * (1.0 / CELLS)
    part_re = [partners[:, 16 * j : 16 * j + 8].astype(jnp.float32).reshape(ROWS, 128) for j in range(OCC)]
    part_im = [partners[:, 16 * j + 8 : 16 * j + 16].astype(jnp.float32).reshape(ROWS, 128) for j in range(OCC)]

    def twisted(re, im):
        return re * twist[0] + im * twist[1], im * twist[0] - re * twist[1]

    sums = {}
    for i in range(BANDS):
        targ_re = targets[2 * i].astype(jnp.float32)
        targ_im = targets[2 * i + 1].astype(jnp.float32)
        top = jnp.concatenate([part_re[j] * targ_re + part_im[j] * targ_im for j in range(OCC)], 1)
        bottom = jnp.concatenate([part_re[j] * targ_im - part_im[j] * targ_re for j in range(OCC)], 1)
        blocks = product(left[...], jnp.concatenate([top, bottom], 0).astype(jnp.bfloat16))
        rows = []
        for j in range(OCC):
            cut = slice(128 * j, 128 * j + 128)
            pair = twisted(blocks[:ROWS, cut], blocks[ROWS:, cut])
            rows.append(jnp.concatenate(pair, 1).astype(jnp.bfloat16))
        tops, bottoms = [], []
        for j in range(OCC):
            spectrum = product(rows[j], right[...])
            scaled = jnp.concatenate([spectrum[:, :128] * kernel[...], spectrum[:, 128:] * -kernel[...]], 1)
            back = product(scaled.astype(jnp.bfloat16), right[...])
            re, im = twisted(back[:, :128], back[:, 128:])
            tops.append(re)
            bottoms.append(im)
        stacked = jnp.concatenate([jnp.concatenate(tops, 1), jnp.concatenate(bottoms, 1)], 0)
        conjugate = product(left[...], stacked.astype(jnp.bfloat16))
        field_re = jnp.zeros((ROWS, 128), jnp.float32)
        field_im = jnp.zeros((ROWS, 128), jnp.float32)
        for j in range(OCC):
            cut = slice(128 * j, 128 * j + 128)
            re, im = conjugate[:ROWS, cut], conjugate[ROWS:, cut]
            field_re -= part_re[j] * re + part_im[j] * im
            field_im += part_re[j] * im - part_im[j] * re
        out[:, 32 * i : 32 * i + 16] = field_re.astype(jnp.bfloat16).reshape(16, 16, 128)
        out[:, 32 * i + 16 : 32 * i + 32] = field_im.astype(jnp.bfloat16).reshape(16, 16, 128)
        for other in range(i + 1):
            base_re = targets[2 * other].astype(jnp.float32)
            base_im = targets[2 * other + 1].astype(jnp.float32)
            same = base_re * field_re + base_im * field_im
            sums[other, i, 0] = same.reshape(GRID, 8, 128).sum(0)
            if other < i:
                cross = base_im * field_re - base_re * field_im
                sums[other, i, 1] = cross.reshape(GRID, 8, 128).sum(0)
    keys = [(i, j, 0) for i, j in PAIRS] + [(i, j, 1) for i, j in PAIRS if i < j]
    totals = jnp.concatenate([jnp.sum(sums[key], 0, keepdims=True) for key in keys], 0)
    totals = jnp.broadcast_to(jnp.sum(totals, 1, keepdims=True), (16, 128))
    lane = lax.broadcasted_iota(jnp.int32, (8, 128), 1)
    value = jnp.where(lane < 64, totals[:8], totals[8:])
    high = value.astype(jnp.bfloat16).astype(jnp.float32)
    middle = (value - high).astype(jnp.bfloat16).astype(jnp.float32)
    low = value - high - middle
    piece = lane % 64 // 16
    value = jnp.where(piece == 0, high, jnp.where(piece == 1, middle, jnp.where(piece == 2, low, 0.0)))
    out[:, 32 * BANDS :] = jnp.broadcast_to(value.astype(jnp.bfloat16)[None], (16, EXTRA, 128))


def exchange(offset, shift, targets, partners):
    left, right, twist = (jnp.asarray(table) for table in tables())
    smem = pl.BlockSpec(memory_space=pltpu.SMEM)
    vmem = pl.BlockSpec(memory_space=pltpu.VMEM)
    return pl.pallas_call(
        exchange_kernel,
        out_shape=jax.ShapeDtypeStruct((16, 32 * BANDS + EXTRA, 128), jnp.bfloat16),
        in_specs=[smem, smem, vmem, vmem, vmem, vmem, vmem],
        out_specs=vmem,
        scratch_shapes=[pltpu.VMEM((ROWS, 128), jnp.float32)],
        compiler_params=pltpu.CompilerParams(vmem_limit_bytes=24 << 20),
        name="exchange",
    )(offset, shift, targets, partners, left, right, twist)


def projector_kernel(shares, out):
    total = shares[0].astype(jnp.float32)
    for source in range(1, 16):
        total += shares[source].astype(jnp.float32)
    values = total[32 * BANDS :]
    values = values + pltpu.roll(values, 112, 1) + pltpu.roll(values, 96, 1)
    values = values * (-1.0 / CELLS)
    count = len(PAIRS)
    keys = [(i, j, 0) for i, j in PAIRS] + [(i, j, 1) for i, j in PAIRS if i < j]
    value = {}
    for at, key in enumerate(keys):
        lane = 64 * (at // 8)
        value[key] = jnp.broadcast_to(values[at % 8 : at % 8 + 1, lane : lane + 1], (8, 128))

    def entry(row, column):
        i, j = row % BANDS, column % BANDS
        if row // BANDS == column // BANDS:
            return value[min(i, j), max(i, j), 0]
        if i == j:
            return None
        return -value[i, j, 1] if i < j else value[j, i, 1]

    size = 2 * BANDS
    factor, inverse = {}, {}
    for column in range(size):
        for row in range(column, size):
            rest = entry(row, column)
            for before in range(column):
                if (row, before) in factor and (column, before) in factor:
                    part = factor[row, before] * factor[column, before]
                    rest = -part if rest is None else rest - part
            if row == column:
                guess = lax.rsqrt(rest)
                inverse[row] = guess * (1.5 - 0.5 * rest * guess * guess)
            elif rest is not None:
                factor[row, column] = rest * inverse[column]
    solved = []
    for row in range(size):
        for_parts = []
        for part in range(2):
            at = 32 * (row % BANDS) + 16 * (part if row < BANDS else 1 - part)
            rest = total[at : at + 16].reshape(2, 8, 128)
            if row >= BANDS and part == 0:
                rest = -rest
            for before in range(row):
                if (row, before) in factor:
                    rest = rest - factor[row, before][None] * solved[before][part]
            rest = rest * inverse[row][None]
            for_parts.append(rest)
            out[pl.ds(32 * row + part, 16, 2), :] = rest.reshape(16, 128)
        solved.append(for_parts)


def projector(shares):
    vmem = pl.BlockSpec(memory_space=pltpu.VMEM)
    return pl.pallas_call(
        projector_kernel,
        out_shape=jax.ShapeDtypeStruct((256, 128), jnp.float32),
        in_specs=[vmem],
        out_specs=vmem,
        compiler_params=pltpu.CompilerParams(vmem_limit_bytes=4 << 20),
        name="projector",
    )(shares)


def local(targets, partners, pair_map, shifts):
    plane = partners.reshape(1, 4 * PLANE, 128)
    gathered = lax.all_to_all(
        jnp.broadcast_to(plane, (GRID, 4 * PLANE, 128)), "ka", 0, 0, tiled=True
    )
    shares = exchange(pair_map, shifts, targets.reshape(2 * BANDS, ROWS, 128), gathered)
    shares = lax.all_to_all(shares, "pb", 0, 0, tiled=True)
    rows = projector(shares).reshape(2 * BANDS, 16, 2, 128)
    return jnp.swapaxes(rows, 1, 2).reshape(1, 2 * BANDS, 2, 2048)


def solution(mesh):
    return jax.shard_map(
        local,
        mesh=mesh,
        in_specs=(
            P("ka", None, None, None),
            P("pb", None, None, "ka"),
            P("ka", "pb"),
            P("ka", "pb", None),
        ),
        out_specs=P("ka", None, None, "pb"),
        check_vma=False,
    )
```

time: 182 us -> 59.6 us (0.33)
  waiting for transfers between devices: 61.7 us -> 11.1 us
  local copies, waits for them, and re-layouts: 40.9 us -> 1.93 us
  blocking collectives: 0 us -> 31 us
  other arithmetic: 28.3 us -> 0 us
  starting transfers between devices: 35.1 us -> 9.32 us
  matrix products: 11.8 us -> 0 us
  Pallas kernels: 0 us -> 5.2 us
  between operations: 2.81 us -> 0.72 us
    all_to_all x6 -> x1, waiting for transfers between devices: 61.7 us -> 11.1 us  [local(): lax.all_to_all(jnp.broadcast_to(plane, (GRID, 4 * PLANE, 128)), 'ka', 0,...]
    all_to_all x0 -> x1, blocking collectives: none -> 31 us  [local(): shares = lax.all_to_all(shares, 'pb', 0, 0, tiled=True)]
    all_to_all x6 -> x1, starting transfers between devices: 35.1 us -> 9.32 us  [local(): lax.all_to_all(jnp.broadcast_to(plane, (GRID, 4 * PLANE, 128)), 'ka', 0,...]
    convert_element_type x8 -> x0, local copies, waits for them, and re-layouts: 17.7 us -> none  [the longest x4 8.86 us: band_field(): blocks = transform(inverse, blocks, FORMS[2]).astype(jnp.bfloat16)]
    mul x8 -> x0, local copies, waits for them, and re-layouts: 15.6 us -> none  [band_field(): transform(inverse, blocks, FORMS[0]).reshape(-1, 2, cells) * (1.0 / cells)]
    dot_general x13 -> x0, matrix products: 11.5 us -> none  [the longest x12 10.3 us: transform(): jnp.einsum(form, exchange_matrix, blocks, preferred_element_type=jnp.floa...]
    another operation x14 -> x0, other arithmetic: 11.4 us -> none
    reduce_sum x9 -> x0, other arithmetic: 6.32 us -> none  [the longest x4 5.83 us: band_field(): jnp.sum(part_re * pot_re - part_im * pot_im, 0)]
  transfers between devices with their start and end apart: 6 -> 1, of which waited for: 6 -> 1; matrix products, arithmetic and copies ran while one was open for 0% -> 1% of each run, Pallas kernels for 0% -> 0%
where the time goes in v1:
time: 59.6 us; the launch traced here: 59.3 us
  blocking collectives  31 us (52%)
  waiting for transfers between devices  11.1 us (19%)
  starting transfers between devices  9.32 us (16%)
  Pallas kernels  5.2 us (9%)
  local copies, waits for them, and re-layouts  1.93 us (3%)
  between operations  0.72 us (1%)
    all_to_all x1, blocking collectives, local(): shares = lax.all_to_all(shares, 'pb', 0, 0, tiled=True)  31 us
    all_to_all x1, waiting for transfers between devices, local(): lax.all_to_all(jnp.broadcast_to(plane, (GRID, 4 * PLANE, 128)), 'ka', 0,...  11.1 us
    all_to_all x1, starting transfers between devices, local(): lax.all_to_all(jnp.broadcast_to(plane, (GRID, 4 * PLANE, 128)), 'ka', 0,...  9.32 us
    pallas_call x1, Pallas kernels, exchange(): pl.pallas_call(exchange_kernel, out_shape=jax.ShapeDtypeStruct((16, 32 *...  4.27 us
    broadcast_in_dim x2, local copies, waits for them, and re-layouts, local(): jnp.broadcast_to(plane, (GRID, 4 * PLANE, 128))  1.51 us
  transfers between devices with their start and end apart: 1, of which 1 were waited for; matrix products, arithmetic and copies ran while one was open for 1% of the time, Pallas kernels for 0%

profile of v1, /device:TPU:8, one launch (start us, length us, event | category | flops | bytes accessed | tf_op | source)
XLA Modules:
  0.0 59.3 jit_solution(13677512640925276058)
XLA Ops:
  0.0 0.0 copy-start.4
  0.0 0.8 %broadcast_in_dim.7 = bf16[32,128]{1,0:T(8,128)(2,1)S(1)} reshape(bf16[1,2,2,1024]{3,2,1,0:T(2,128)(2,1)} %param.8) | data formatting | bytes 16384 | tf_op jit(solution)/shard_map/broadcast_in_dim | solution.py:203
  0.8 0.7 %broadcast_in_dim.8 = bf16[32,32,128]{2,1,0:T(8,128)(2,1)} broadcast(bf16[32,128]{1,0:T(8,128)(2,1)S(1)} %broadcast_in_dim.7), dimensions={1,2} | broadcast | bytes 270336 | tf_op jit(solution)/shard_map/broadcast_in_dim | solution.py:203
  1.5 9.3 %all-to-all-start = ((bf16[32,32,128]{2,1,0:T(8,128)(2,1)}), bf16[32,32,128]{2,1,0:T(8,128)(2,1)S(1)}, u32[]{:S(2)}, u32[]{:S(2)}) async-start(bf16[32,32,128]{2,1,0:T(8,128)(2,1)} %broadcast_in_dim.8), calls=%async_computation | async-start | bytes 524288 | tf_op jit(solution)/shard_map/all_to_all | solution.py:202
  11.5 0.0 copy-done.4
  11.5 0.0 copy-start
  11.5 0.0 copy-start.1
  11.5 0.0 copy-start.2
  11.5 0.0 copy-start.3
  11.5 0.4 reshape.11.targets
  11.9 11.1 %all-to-all-done.partners = bf16[32,32,128]{2,1,0:T(8,128)(2,1)S(1)} async-done(((bf16[32,32,128]{2,1,0:T(8,128)(2,1)}), bf16[32,32,128]{2,1,0:T(8,128)(2,1)S(1)}, u32[]{:S(2)}, u32[]{:S(2)}) %all-to-all-start) | async-done | bytes 262176 | tf_op jit(solution)/shard_map/all_to_all | solution.py:202
  23.1 0.0 copy-done
  23.1 0.0 copy-done.1
  23.1 0.0 copy-done.2
  23.1 0.0 copy-done.3
  23.1 4.3 %exchange.1 = bf16[16,136,128]{2,1,0:T(8,128)(2,1)S(1)} custom-call(s32[1,1]{1,0:T(1,128)S(6)} %copy.9.offset, s32[1,1,3]{2,1,0:T(1,128)S(1)} %copy-done.3, bf16[8,256,128]{2,1,0:T(8,128)(2,1)S(1)} %reshape.11.targets, bf16[32,32,128]{2,1,0:T(8,128)(2,1)S(1)} %all-to-all-done.partners, bf16[512,512]{1,0:T(8,128)(2,1)S(1)} %copy-done, ...), custom_call_target="tpu_custom_call" | custom-call | tf_op jit(solution)/shard_map/exchange/pallas_call | solution.py:124
  27.4 31.0 %all_to_all.10.shares = bf16[16,136,128]{2,1,0:T(8,128)(2,1)S(1)} all-to-all(bf16[16,136,128]{2,1,0:T(8,128)(2,1)S(1)} %exchange.1), channel_id=1, replica_groups=mesh['ka'=32,'pb'=16] {'pb'}, dimensions={0} | all-to-all | bytes 1114112 | tf_op jit(solution)/shard_map/all_to_all | solution.py:206
  58.3 0.9 %projector.1 = f32[256,128]{1,0:T(8,128)} custom-call(bf16[16,136,128]{2,1,0:T(8,128)(2,1)S(1)} %all_to_all.10.shares), custom_call_target="tpu_custom_call" | custom-call | tf_op jit(solution)/shard_map/projector/pallas_call | solution.py:190
Async XLA Ops:
  0.0 11.5 %copy-start.4 = (bf16[1,4,2,32768]{3,2,1,0:T(2,128)(2,1)S(1)}, bf16[1,4,2,32768]{3,2,1,0:T(2,128)(2,1)}, u32[]{:S(2)}) copy-start(bf16[1,4,2,32768]{3,2,1,0:T(2,128)(2,1)} %param.7) | copy-start | bytes 1572868
  1.5 21.5 %all-to-all-start = ((bf16[32,32,128]{2,1,0:T(8,128)(2,1)}), bf16[32,32,128]{2,1,0:T(8,128)(2,1)S(1)}, u32[]{:S(2)}, u32[]{:S(2)}) async-start(bf16[32,32,128]{2,1,0:T(8,128)(2,1)} %broadcast_in_dim.8), calls=%async_computation | async-start | bytes 524288 | tf_op jit(solution)/shard_map/all_to_all | solution.py:202
  11.5 11.6 %copy-start = (bf16[512,512]{1,0:T(8,128)(2,1)S(1)}, bf16[512,512]{1,0:T(8,128)(2,1)}, u32[]{:S(2)}) copy-start(bf16[512,512]{1,0:T(8,128)(2,1)} %constant.6.clone.left) | copy-start | bytes 1572868
  11.5 11.6 %copy-start.1 = (f32[2,256,128]{2,1,0:T(8,128)S(1)}, f32[2,256,128]{2,1,0:T(8,128)}, u32[]{:S(2)}) copy-start(f32[2,256,128]{2,1,0:T(8,128)} %constant.8.clone.twist) | copy-start | bytes 786436
  11.5 11.5 %copy-start.2 = (bf16[256,256]{1,0:T(8,128)(2,1)S(1)}, bf16[256,256]{1,0:T(8,128)(2,1)}, u32[]{:S(2)}) copy-start(bf16[256,256]{1,0:T(8,128)(2,1)} %constant.7.clone.right) | copy-start | bytes 393220
  11.5 11.5 %copy-start.3 = (s32[1,1,3]{2,1,0:T(1,128)S(1)}, s32[1,1,3]{2,1,0:T(1,128)}, u32[]{:S(2)}) copy-start(s32[1,1,3]{2,1,0:T(1,128)} %shift.1) | copy-start | bytes 40

commit v2 on v1

v2 whole, which is shorter than its diff:
```python
import jax
import jax.numpy as jnp
import numpy as np
from jax import lax
from jax.experimental import pallas as pl
from jax.experimental.pallas import tpu as pltpu
from jax.sharding import Mesh
from jax.sharding import PartitionSpec as P

GRID = 32
BANDS = 4
OWN = 2
PLANE = 8
ROWS = GRID * PLANE
CELLS = GRID**3
KPOINT_SCALING = 2.0
SCREENING_CUTOFF = 0.25
FIELD_ROWS = 32 * OWN
EXTRA = 8


def phases(angle):
    turn = 2.0 * np.pi * (angle % GRID) / GRID
    return np.cos(turn), np.sin(turn)


def tables():
    row = np.arange(ROWS)
    lane = np.arange(128)
    hi, lo = row // PLANE, row % PLANE
    cos, sin = phases(hi[:, None] * hi[None] + 4 * lo[:, None] * lo[None])
    left = np.block([[cos, sin], [-sin, cos]])
    part, z = lane // GRID, lane % GRID
    cos, sin = phases(z[:, None] * z[None] + 8 * part[:, None] * part[None])
    right = np.block([[cos, -sin], [sin, cos]])
    twist = np.stack(phases(lo[:, None] * part[None]))
    return left.astype(jnp.bfloat16), right.astype(jnp.bfloat16), twist.astype(np.float32)


def wave_number(index):
    return ((index + GRID // 2) % GRID - GRID // 2).astype(jnp.float32)


def coulomb(offset, shift):
    row = lax.broadcasted_iota(jnp.int32, (ROWS, 128), 0)
    lane = lax.broadcasted_iota(jnp.int32, (ROWS, 128), 1)
    index = (row // PLANE, (lane // GRID) * PLANE + row % PLANE, lane % GRID)
    lattice = (offset // 16, offset // 4 % 4, offset % 4)
    squared = jnp.zeros((ROWS, 128), jnp.float32)
    for axis in range(3):
        moved = shift[axis].astype(jnp.float32) + lattice[axis].astype(jnp.float32) * 0.25
        component = wave_number(index[axis]) + moved
        squared += component * component
    return KPOINT_SCALING / (squared + SCREENING_CUTOFF)


def product(a, b):
    return jnp.dot(a, b, preferred_element_type=jnp.float32)


def spread_kernel(plane, out):
    out[...] = jnp.broadcast_to(plane[...][None], out.shape)


def prepare_kernel(mine, theirs, targets, kernel, parts, rows):
    place = mine[0, 4]
    for q in range(2):
        number = [jnp.where(place == q, mine[0, at], theirs[0, at]) for at in range(4)]
        kernel[q] = coulomb(number[0], number[1:]) * (1.0 / CELLS)
    for slot in range(BANDS):
        rows[...] = targets[(2 * place + slot) % BANDS].astype(jnp.float32)
        for part in range(2):
            parts[slot, part] = rows[pl.ds(part, ROWS, 2), :]


def fields_of(kernel, targets, gathered, left, right, twist, rows, parts):
    rows[...] = gathered[...].astype(jnp.float32).reshape(4 * ROWS, 128)
    for q in range(2):
        for part in range(2):
            parts[q, part] = rows[pl.ds(2 * ROWS * q + part, ROWS, 2), :]

    def twisted(re, im):
        return re * twist[0] + im * twist[1], im * twist[0] - re * twist[1]

    for band in range(OWN):
        tops, bottoms = [], []
        for q in range(2):
            tops.append(parts[q, 0] * targets[band, 0] + parts[q, 1] * targets[band, 1])
            bottoms.append(parts[q, 0] * targets[band, 1] - parts[q, 1] * targets[band, 0])
        density = jnp.concatenate([jnp.concatenate(tops, 1), jnp.concatenate(bottoms, 1)], 0)
        blocks = product(left[...], density.astype(jnp.bfloat16))
        tops, bottoms = [], []
        for q in range(2):
            cut = slice(128 * q, 128 * q + 128)
            pair = twisted(blocks[:ROWS, cut], blocks[ROWS:, cut])
            spectrum = product(jnp.concatenate(pair, 1).astype(jnp.bfloat16), right[...])
            scaled = jnp.concatenate(
                [spectrum[:, :128] * kernel[q], spectrum[:, 128:] * -kernel[q]], 1
            )
            back = product(scaled.astype(jnp.bfloat16), right[...])
            re, im = twisted(back[:, :128], back[:, 128:])
            tops.append(re)
            bottoms.append(im)
        stacked = jnp.concatenate([jnp.concatenate(tops, 1), jnp.concatenate(bottoms, 1)], 0)
        conjugate = product(left[...], stacked.astype(jnp.bfloat16))
        re_sum, im_sum = None, None
        for q in range(2):
            cut = slice(128 * q, 128 * q + 128)
            re, im = conjugate[:ROWS, cut], conjugate[ROWS:, cut]
            re_now = -(parts[q, 0] * re) - parts[q, 1] * im
            im_now = parts[q, 0] * im - parts[q, 1] * re
            re_sum = re_now if re_sum is None else re_sum + re_now
            im_sum = im_now if im_sum is None else im_sum + im_now
        yield band, re_sum, im_sum


def first_kernel(kernel, targets, gathered, left, right, twist, out, rows, parts):
    for band, re, im in fields_of(kernel, targets, gathered, left, right, twist, rows, parts):
        out[band, 0] = re
        out[band, 1] = im


def second_kernel(kernel, targets, gathered, left, right, twist, before, out, rows, parts):
    same, cross = {}, {}
    for band, re, im in fields_of(kernel, targets, gathered, left, right, twist, rows, parts):
        re += before[band, 0]
        im += before[band, 1]
        out[:, 32 * band : 32 * band + 16] = re.astype(jnp.bfloat16).reshape(16, 16, 128)
        out[:, 32 * band + 16 : 32 * band + 32] = im.astype(jnp.bfloat16).reshape(16, 16, 128)
        for slot in range(BANDS):
            total = targets[slot, 0] * re + targets[slot, 1] * im
            same[slot, band] = total.reshape(GRID, 8, 128).sum(0)
            total = targets[slot, 1] * re - targets[slot, 0] * im
            cross[slot, band] = total.reshape(GRID, 8, 128).sum(0)
    keys = [(slot, band) for slot in range(BANDS) for band in range(OWN)]
    totals = [jnp.sum(group[key], 0, keepdims=True) for group in (same, cross) for key in keys]
    totals = jnp.sum(jnp.concatenate(totals, 0), 1, keepdims=True)
    totals = jnp.broadcast_to(totals, (16, 128))
    lane = lax.broadcasted_iota(jnp.int32, (8, 128), 1)
    value = jnp.where(lane < 64, totals[:8], totals[8:])
    high = value.astype(jnp.bfloat16).astype(jnp.float32)
    middle = (value - high).astype(jnp.bfloat16).astype(jnp.float32)
    low = value - high - middle
    piece = lane % 64 // 16
    value = jnp.where(piece == 0, high, jnp.where(piece == 1, middle, jnp.where(piece == 2, low, 0.0)))
    out[:, FIELD_ROWS:] = jnp.broadcast_to(value.astype(jnp.bfloat16)[None], (16, EXTRA, 128))


def projector_kernel(shares, out):
    totals = []
    for group in range(2):
        total = shares[8 * group].astype(jnp.float32)
        for source in range(8 * group + 1, 8 * group + 8):
            total += shares[source].astype(jnp.float32)
        totals.append(total)
    same, cross = {}, {}
    for group in range(2):
        values = totals[group][FIELD_ROWS:]
        values = values + pltpu.roll(values, 112, 1) + pltpu.roll(values, 96, 1)
        values = values * (1.0 / CELLS)
        for slot in range(BANDS):
            for band in range(OWN):
                at = OWN * slot + band
                key = (2 * group + slot) % BANDS, 2 * group + band
                same[key] = jnp.broadcast_to(values[at : at + 1, 0:1], (8, 128))
                cross[key] = jnp.broadcast_to(values[at : at + 1, 64:65], (8, 128))

    def entry(row, column):
        i, j = row % BANDS, column % BANDS
        if row // BANDS == column // BANDS:
            return -0.5 * (same[i, j] + same[j, i])
        return None if i == j else 0.5 * (cross[i, j] - cross[j, i])

    size = 2 * BANDS
    factor, inverse = {}, {}
    for column in range(size):
        for row in range(column, size):
            rest = entry(row, column)
            for before in range(column):
                if (row, before) in factor and (column, before) in factor:
                    part = factor[row, before] * factor[column, before]
                    rest = -part if rest is None else rest - part
            if row == column:
                guess = lax.rsqrt(rest)
                inverse[row] = guess * (1.5 - 0.5 * rest * guess * guess)
            elif rest is not None:
                factor[row, column] = rest * inverse[column]
    solved = []
    for row in range(size):
        for_parts = []
        for part in range(2):
            band = row % BANDS
            at = 32 * (band % OWN) + 16 * (part if row < BANDS else 1 - part)
            rest = totals[band // OWN][at : at + 16].reshape(2, 8, 128)
            if row >= BANDS and part == 0:
                rest = -rest
            for before in range(row):
                if (row, before) in factor:
                    rest = rest - factor[row, before][None] * solved[before][part]
            rest = rest * inverse[row][None]
            for_parts.append(rest)
            out[pl.ds(32 * row + part, 16, 2), :] = rest.reshape(16, 128)
        solved.append(for_parts)


SMEM = pl.BlockSpec(memory_space=pltpu.SMEM)
VMEM = pl.BlockSpec(memory_space=pltpu.VMEM)


def call(kernel, name, shapes, specs, scratch, limit, *operands):
    return pl.pallas_call(
        kernel,
        out_shape=shapes,
        in_specs=specs,
        out_specs=jax.tree.map(lambda _: VMEM, shapes),
        scratch_shapes=scratch,
        compiler_params=pltpu.CompilerParams(vmem_limit_bytes=limit << 20),
        name=name,
    )(*operands)


def array(*shape, dtype=jnp.float32):
    return jax.ShapeDtypeStruct(shape, dtype)


def spread(plane):
    shape = array(GRID, 4 * PLANE, 128, dtype=jnp.bfloat16)
    return call(spread_kernel, "spread", shape, [VMEM], [], 1, plane)


def prepare(mine, theirs, targets):
    shapes = (array(2, ROWS, 128), array(BANDS, 2, ROWS, 128))
    scratch = [pltpu.VMEM((2 * ROWS, 128), jnp.float32)]
    return call(prepare_kernel, "prepare", shapes, [SMEM, SMEM, VMEM], scratch, 8, mine, theirs, targets)


def exchange(*operands):
    scratch = [pltpu.VMEM((4 * ROWS, 128), jnp.float32), pltpu.VMEM((2, 2, ROWS, 128), jnp.float32)]
    specs = [VMEM] * len(operands)
    if len(operands) == 6:
        return call(first_kernel, "first", array(OWN, 2, ROWS, 128), specs, scratch, 16, *operands)
    shape = array(16, FIELD_ROWS + EXTRA, 128, dtype=jnp.bfloat16)
    return call(second_kernel, "second", shape, specs, scratch, 16, *operands)


def projector(shares):
    return call(projector_kernel, "projector", array(256, 128), [VMEM], [], 4, shares)


def interleaved(values):
    tiles = values.reshape(values.shape[0], 2, values.shape[2] // 128, 128)
    return jnp.swapaxes(tiles, 1, 2).reshape(values.shape[0], -1, 128)


def local(targets, partners, pair_map, shifts):
    left, right, twist = (jnp.asarray(table) for table in tables())
    place = lax.axis_index("xh")
    operand = spread(interleaved(partners[0]).reshape(4 * PLANE, 128)).reshape(2 * GRID, 2 * PLANE, 128)
    gathered = lax.all_to_all(operand, ("xh", "ka"), 0, 0, tiled=True)
    mine = jnp.concatenate([pair_map, shifts[0], place.reshape(1, 1)], 1)
    theirs = lax.ppermute(mine, "xh", [(0, 1), (1, 0)])
    kernel, parts = prepare(mine, theirs, interleaved(targets[0]))
    gathered, kernel, parts = lax.optimization_barrier((gathered, kernel, parts))
    count = lax.axis_size("ka")
    swapped = lax.ppermute(gathered, "ka", [(i, i ^ 1) for i in range(count)])
    before = exchange(kernel, parts, gathered, left, right, twist)
    shares = exchange(kernel, parts, swapped, left, right, twist, before)
    shares = lax.all_to_all(shares, ("xh", "zz"), 0, 0, tiled=True)
    rows = projector(shares).reshape(2 * BANDS, 16, 2, 128)
    return jnp.swapaxes(rows, 1, 2).reshape(1, 2 * BANDS, 2, 2048)


def solution(mesh):
    split = Mesh(mesh.devices.reshape(GRID, 2, 8), ("ka", "xh", "zz"))
    return jax.shard_map(
        local,
        mesh=split,
        in_specs=(
            P("ka", None, None, None),
            P(("xh", "zz"), None, None, "ka"),
            P("ka", ("xh", "zz")),
            P("ka", ("xh", "zz"), None),
        ),
        out_specs=P("ka", None, None, ("xh", "zz")),
        check_vma=False,
    )
```

time: 59.6 us -> 56.2 us (0.943)
  the two profiles are of different devices: /device:TPU:8 before, /device:TPU:1 now
where the time goes in v2:
time: 56.2 us; the launch traced here: 55.7 us
  blocking collectives  23.1 us (41%)
  starting transfers between devices  19 us (34%)
  Pallas kernels  6.69 us (12%)
  waiting for transfers between devices  3.73 us (7%)
  local copies, waits for them, and re-layouts  2.4 us (4%)
  between operations  0.74 us (1%)
    all_to_all x1, blocking collectives, local(): shares = lax.all_to_all(shares, ('xh', 'zz'), 0, 0, tiled=True)  23.1 us
    all_to_all x1, starting transfers between devices, local(): gathered = lax.all_to_all(operand, ('xh', 'ka'), 0, 0, tiled=True)  11.7 us
    pallas_call x5, Pallas kernels, call(): pl.pallas_call(kernel, out_shape=shapes, in_specs=specs, out_specs=jax.tr...  6.69 us
    ppermute x1, starting transfers between devices, local(): theirs = lax.ppermute(mine, 'xh', [(0, 1), (1, 0)])  4.86 us
    all_to_all x1, waiting for transfers between devices, local(): gathered = lax.all_to_all(operand, ('xh', 'ka'), 0, 0, tiled=True)  2.49 us
    unnamed x12, local copies, waits for them, and re-layouts  2.4 us
    ppermute x1, starting transfers between devices, local(): swapped = lax.ppermute(gathered, 'ka', [(i, i ^ 1) for i in range(count)])  2.36 us
    ppermute x1, waiting for transfers between devices, local(): theirs = lax.ppermute(mine, 'xh', [(0, 1), (1, 0)])  1.24 us
  transfers between devices with their start and end apart: 3, of which 2 were waited for; matrix products, arithmetic and copies ran while one was open for 0% of the time, Pallas kernels for 5%

profile of v2, /device:TPU:1, one launch (start us, length us, event | category | flops | bytes accessed | tf_op | source)
XLA Modules:
  0.0 55.7 jit_solution(10642325678894648898)
XLA Ops:
  0.0 0.0 copy-start.4
  0.0 0.7 %copy-done.4 = bf16[1,2,2,1024]{3,2,1,0:T(2,128)(2,1)S(1)} copy-done((bf16[1,2,2,1024]{3,2,1,0:T(2,128)(2,1)S(1)}, bf16[1,2,2,1024]{3,2,1,0:T(2,128)(2,1)}, u32[]{:S(2)}) %copy-start.4) | copy-done | bytes 8216
  0.7 0.7 %spread.1 = bf16[32,32,128]{2,1,0:T(8,128)(2,1)} custom-call(bf16[32,128]{1,0:T(8,128)(2,1)S(1)} %bitcast.19), custom_call_target="tpu_custom_call" | custom-call | tf_op jit(solution)/shard_map/spread/pallas_call | solution.py:211
  1.4 0.0 copy-start
  1.4 11.7 %all-to-all-start = ((bf16[64,16,128]{2,1,0:T(8,128)(2,1)}), bf16[64,16,128]{2,1,0:T(8,128)(2,1)S(1)}, u32[]{:S(2)}, u32[]{:S(2)}) async-start(bf16[64,16,128]{2,1,0:T(8,128)(2,1)} %bitcast.3), calls=%async_computation | async-start | bytes 524288 | tf_op jit(solution)/shard_map/all_to_all | solution.py:259
  13.8 0.0 copy-start.5
  13.9 0.6 %copy-done.5 = s32[1,1,3]{2,1,0:T(1,128)S(1)} copy-done((s32[1,1,3]{2,1,0:T(1,128)S(1)}, s32[1,1,3]{2,1,0:T(1,128)}, u32[]{:S(2)}) %copy-start.5) | copy-done | bytes 36
  14.5 0.1 pad_add_fusion.mine
  14.6 4.9 %collective-permute-start = (s32[1,5]{1,0:T(1,128)S(1)}, s32[1,5]{1,0:T(1,128)S(1)}, u32[]{:S(2)}, u32[]{:S(2)}) collective-permute-start(s32[1,5]{1,0:T(1,128)S(1)} %pad_add_fusion.mine), channel_id=1, source_target_pairs={{0,8},{8,0},{1,9},{9,1},{2,10},{10,2},{3,11},{11,3},{4,12},{12,4},... | collective-permute-start | bytes 68 | tf_op jit(solution)/shard_map/ppermute | solution.py:261
  19.4 1.2 %collective-permute-done.theirs = s32[1,5]{1,0:T(1,128)S(1)} collective-permute-done((s32[1,5]{1,0:T(1,128)S(1)}, s32[1,5]{1,0:T(1,128)S(1)}, u32[]{:S(2)}, u32[]{:S(2)}) %collective-permute-start) | collective-permute-done | bytes 52 | tf_op jit(solution)/shard_map/ppermute | solution.py:261
  20.7 0.0 copy-start.3
  20.7 1.0 %copy-done.3 = bf16[1,4,2,32768]{3,2,1,0:T(2,128)(2,1)S(1)} copy-done((bf16[1,4,2,32768]{3,2,1,0:T(2,128)(2,1)S(1)}, bf16[1,4,2,32768]{3,2,1,0:T(2,128)(2,1)}, u32[]{:S(2)}) %copy-start.3) | copy-done | bytes 524312
  21.7 0.0 copy-start.1
  21.7 0.0 copy-start.2
  21.7 0.9 %prepare.1 = (f32[2,256,128]{2,1,0:T(8,128)S(1)}, f32[4,2,256,128]{3,2,1,0:T(8,128)S(1)}) custom-call(s32[1,5]{1,0:T(1,128)S(1)} %pad_add_fusion.mine, s32[1,5]{1,0:T(1,128)S(1)} %collective-permute-done.theirs, bf16[4,512,128]{2,1,0:T(8,128)(2,1)S(1)} %bitcast.18), custom_call_target="tpu_custom_call" | custom-call | tf_op jit(solution)/shard_map/prepare/pallas_call | solution.py:211
  22.7 2.5 %all-to-all-done.gathered = bf16[64,16,128]{2,1,0:T(8,128)(2,1)S(1)} async-done(((bf16[64,16,128]{2,1,0:T(8,128)(2,1)}), bf16[64,16,128]{2,1,0:T(8,128)(2,1)S(1)}, u32[]{:S(2)}, u32[]{:S(2)}) %all-to-all-start) | async-done | bytes 262176 | tf_op jit(solution)/shard_map/all_to_all | solution.py:259
  25.2 2.4 %collective-permute-start.1 = (bf16[64,16,128]{2,1,0:T(8,128)(2,1)S(1)}, bf16[64,16,128]{2,1,0:T(8,128)(2,1)S(1)}, u32[]{:S(2)}, u32[]{:S(2)}) collective-permute-start(bf16[64,16,128]{2,1,0:T(8,128)(2,1)S(1)} %all-to-all-done.gathered), channel_id=1, source_target_pairs={{0,16},{16,0},{32,48},{48,32},{64,80},{80,64},{96,112},{112,96},{1... | collective-permute-start | bytes 786440 | tf_op jit(solution)/shard_map/ppermute | solution.py:265
  27.5 0.0 copy-done
  27.5 0.0 copy-done.1
  27.5 0.0 copy-done.2
  27.6 1.8 %first.1.before = f32[2,2,256,128]{3,2,1,0:T(8,128)S(1)} custom-call(f32[2,256,128]{2,1,0:T(8,128)S(1)} %get-tuple-element.12.kernel, f32[4,2,256,128]{3,2,1,0:T(8,128)S(1)} %get-tuple-element.13.targets, bf16[64,16,128]{2,1,0:T(8,128)(2,1)S(1)} %all-to-all-done.gathered, bf16[512,512]{1,0:T(8,128)(2,1)S(1)} %copy-done, bf16[256,256]{1,0:T(8,128)(2,1)S(1)} %copy-done.2, ...), custom_call_target="tpu_custom_call" | custom-call | tf_op jit(solution)/shard_map/first/pallas_call | solution.py:211
  29.4 0.0 collective-permute-done.1.gathered
  29.4 2.2 %second.1 = bf16[16,72,128]{2,1,0:T(8,128)(2,1)S(1)} custom-call(f32[2,256,128]{2,1,0:T(8,128)S(1)} %get-tuple-element.12.kernel, f32[4,2,256,128]{3,2,1,0:T(8,128)S(1)} %get-tuple-element.13.targets, bf16[64,16,128]{2,1,0:T(8,128)(2,1)S(1)} %collective-permute-done.1.gathered, bf16[512,512]{1,0:T(8,128)(2,1)S(1)} %copy-done, ...), custom_call_target="tpu_custom_call" | custom-call | tf_op jit(solution)/shard_map/second/pallas_call | solution.py:211
  31.6 23.1 %all_to_all.10.shares = bf16[16,72,128]{2,1,0:T(8,128)(2,1)S(1)} all-to-all(bf16[16,72,128]{2,1,0:T(8,128)(2,1)S(1)} %second.1), channel_id=1, replica_groups=mesh['ka'=32,'xh'=2,'zz'=8] {'xh','zz'}, dimensions={0} | all-to-all | bytes 589824 | tf_op jit(solution)/shard_map/all_to_all | solution.py:268
  54.7 1.0 %projector.1 = f32[256,128]{1,0:T(8,128)} custom-call(bf16[16,72,128]{2,1,0:T(8,128)(2,1)S(1)} %all_to_all.10.shares), custom_call_target="tpu_custom_call" | custom-call | tf_op jit(solution)/shard_map/projector/pallas_call | solution.py:211
Async XLA Ops:
  0.0 0.7 %copy-start.4 = (bf16[1,2,2,1024]{3,2,1,0:T(2,128)(2,1)S(1)}, bf16[1,2,2,1024]{3,2,1,0:T(2,128)(2,1)}, u32[]{:S(2)}) copy-start(bf16[1,2,2,1024]{3,2,1,0:T(2,128)(2,1)} %param.8) | copy-start | bytes 24580
  1.4 26.1 %copy-start = (bf16[512,512]{1,0:T(8,128)(2,1)S(1)}, bf16[512,512]{1,0:T(8,128)(2,1)}, u32[]{:S(2)}) copy-start(bf16[512,512]{1,0:T(8,128)(2,1)} %constant.12.clone.left) | copy-start | bytes 1572868
  1.4 23.7 %all-to-all-start = ((bf16[64,16,128]{2,1,0:T(8,128)(2,1)}), bf16[64,16,128]{2,1,0:T(8,128)(2,1)S(1)}, u32[]{:S(2)}, u32[]{:S(2)}) async-start(bf16[64,16,128]{2,1,0:T(8,128)(2,1)} %bitcast.3), calls=%async_computation | async-start | bytes 524288 | tf_op jit(solution)/shard_map/all_to_all | solution.py:259
  13.8 0.7 %copy-start.5 = (s32[1,1,3]{2,1,0:T(1,128)S(1)}, s32[1,1,3]{2,1,0:T(1,128)}, u32[]{:S(2)}) copy-start(s32[1,1,3]{2,1,0:T(1,128)} %param.10) | copy-start | bytes 40
  14.6 6.1 %collective-permute-start = (s32[1,5]{1,0:T(1,128)S(1)}, s32[1,5]{1,0:T(1,128)S(1)}, u32[]{:S(2)}, u32[]{:S(2)}) collective-permute-start(s32[1,5]{1,0:T(1,128)S(1)} %pad_add_fusion.mine), channel_id=1, source_target_pairs={{0,8},{8,0},{1,9},{9,1},{2,10},{10,2},{3,11},{11,3},{4,12},{12,4},... | collective-permute-start | bytes 68 | tf_op jit(solution)/shard_map/ppermute | solution.py:261
  20.7 1.0 %copy-start.3 = (bf16[1,4,2,32768]{3,2,1,0:T(2,128)(2,1)S(1)}, bf16[1,4,2,32768]{3,2,1,0:T(2,128)(2,1)}, u32[]{:S(2)}) copy-start(bf16[1,4,2,32768]{3,2,1,0:T(2,128)(2,1)} %param.7) | copy-start | bytes 1572868
  21.7 5.8 %copy-start.1 = (f32[2,256,128]{2,1,0:T(8,128)S(1)}, f32[2,256,128]{2,1,0:T(8,128)}, u32[]{:S(2)}) copy-start(f32[2,256,128]{2,1,0:T(8,128)} %constant.14.clone.twist) | copy-start | bytes 786436
  21.7 5.8 %copy-start.2 = (bf16[256,256]{1,0:T(8,128)(2,1)S(1)}, bf16[256,256]{1,0:T(8,128)(2,1)}, u32[]{:S(2)}) copy-start(bf16[256,256]{1,0:T(8,128)(2,1)} %constant.13.clone.right) | copy-start | bytes 393220
  25.2 4.2 %collective-permute-start.1 = (bf16[64,16,128]{2,1,0:T(8,128)(2,1)S(1)}, bf16[64,16,128]{2,1,0:T(8,128)(2,1)S(1)}, u32[]{:S(2)}, u32[]{:S(2)}) collective-permute-start(bf16[64,16,128]{2,1,0:T(8,128)(2,1)S(1)} %all-to-all-done.gathered), channel_id=1, source_target_pairs={{0,16},{16,0},{32,48},{48,32},{64,80},{80,64},{96,112},{112,96},{1... | collective-permute-start | bytes 786440 | tf_op jit(solution)/shard_map/ppermute | solution.py:265

commit v3 on v2

--- a/solution.py
+++ b/solution.py
@@ -17,6 +17,7 @@
 SCREENING_CUTOFF = 0.25
 FIELD_ROWS = 32 * OWN
 EXTRA = 8
+PAIRS = [(0, 0, 0), (1, 1, 0), (0, 1, 0), (0, 1, 1), (2, 0, 0), (2, 0, 1), (3, 1, 0), (3, 1, 1)]
 
 
 def phases(angle):
@@ -58,19 +59,22 @@
     return jnp.dot(a, b, preferred_element_type=jnp.float32)
 
 
-def spread_kernel(plane, out):
-    out[...] = jnp.broadcast_to(plane[...][None], out.shape)
-
-
-def prepare_kernel(mine, theirs, targets, kernel, parts, rows):
+def coulomb_kernel(mine, theirs, kernel):
     place = mine[0, 4]
     for q in range(2):
         number = [jnp.where(place == q, mine[0, at], theirs[0, at]) for at in range(4)]
         kernel[q] = coulomb(number[0], number[1:]) * (1.0 / CELLS)
+
+
+def apart_kernel(place, targets, parts, rows):
     for slot in range(BANDS):
-        rows[...] = targets[(2 * place + slot) % BANDS].astype(jnp.float32)
+        rows[...] = targets[band_of(slot, place[0, 0])].astype(jnp.float32)
         for part in range(2):
             parts[slot, part] = rows[pl.ds(part, ROWS, 2), :]
+
+
+def band_of(slot, place):
+    return 2 * place + slot if slot < OWN else slot - (1 + 2 * (slot - OWN)) * place
 
 
 def fields_of(kernel, targets, gathered, left, right, twist, rows, parts):
@@ -82,27 +86,43 @@
     def twisted(re, im):
         return re * twist[0] + im * twist[1], im * twist[0] - re * twist[1]
 
-    for band in range(OWN):
+    def density(band):
         tops, bottoms = [], []
         for q in range(2):
             tops.append(parts[q, 0] * targets[band, 0] + parts[q, 1] * targets[band, 1])
             bottoms.append(parts[q, 0] * targets[band, 1] - parts[q, 1] * targets[band, 0])
-        density = jnp.concatenate([jnp.concatenate(tops, 1), jnp.concatenate(bottoms, 1)], 0)
-        blocks = product(left[...], density.astype(jnp.bfloat16))
-        tops, bottoms = [], []
+        return joined(tops, bottoms)
+
+    def joined(tops, bottoms):
+        rows = [jnp.concatenate(tops, 1), jnp.concatenate(bottoms, 1)]
+        return jnp.concatenate(rows, 0).astype(jnp.bfloat16)
+
+    def to_spectrum(blocks):
+        pairs = []
         for q in range(2):
             cut = slice(128 * q, 128 * q + 128)
             pair = twisted(blocks[:ROWS, cut], blocks[ROWS:, cut])
-            spectrum = product(jnp.concatenate(pair, 1).astype(jnp.bfloat16), right[...])
-            scaled = jnp.concatenate(
-                [spectrum[:, :128] * kernel[q], spectrum[:, 128:] * -kernel[q]], 1
-            )
-            back = product(scaled.astype(jnp.bfloat16), right[...])
-            re, im = twisted(back[:, :128], back[:, 128:])
+            pairs.append(jnp.concatenate(pair, 1).astype(jnp.bfloat16))
+        return product(jnp.concatenate(pairs, 0), right[...])
+
+    def from_spectrum(spectrum):
+        scaled = []
+        for q in range(2):
+            cut = slice(ROWS * q, ROWS * q + ROWS)
+            pair = spectrum[cut, :128] * kernel[q], spectrum[cut, 128:] * -kernel[q]
+            scaled.append(jnp.concatenate(pair, 1).astype(jnp.bfloat16))
+        return product(jnp.concatenate(scaled, 0), right[...])
+
+    def untwisted(back):
+        tops, bottoms = [], []
+        for q in range(2):
+            cut = slice(ROWS * q, ROWS * q + ROWS)
+            re, im = twisted(back[cut, :128], back[cut, 128:])
             tops.append(re)
             bottoms.append(im)
-        stacked = jnp.concatenate([jnp.concatenate(tops, 1), jnp.concatenate(bottoms, 1)], 0)
-        conjugate = product(left[...], stacked.astype(jnp.bfloat16))
+        return joined(tops, bottoms)
+
+    def field(conjugate):
         re_sum, im_sum = None, None
         for q in range(2):
             cut = slice(128 * q, 128 * q + 128)
@@ -111,7 +131,14 @@
             im_now = parts[q, 0] * im - parts[q, 1] * re
             re_sum = re_now if re_sum is None else re_sum + re_now
             im_sum = im_now if im_sum is None else im_sum + im_now
-        yield band, re_sum, im_sum
+        return re_sum, im_sum
+
+    values = [product(left[...], density(band)) for band in range(OWN)]
+    values = [to_spectrum(value) for value in values]
+    values = [from_spectrum(value) for value in values]
+    values = [product(left[...], untwisted(value)) for value in values]
+    for band, value in enumerate(values):
+        yield (band, *field(value))
 
 
 def first_kernel(kernel, targets, gathered, left, right, twist, out, rows, parts):
@@ -121,27 +148,25 @@
 
 
 def second_kernel(kernel, targets, gathered, left, right, twist, before, out, rows, parts):
-    same, cross = {}, {}
+    sums = {}
     for band, re, im in fields_of(kernel, targets, gathered, left, right, twist, rows, parts):
         re += before[band, 0]
         im += before[band, 1]
         out[:, 32 * band : 32 * band + 16] = re.astype(jnp.bfloat16).reshape(16, 16, 128)
         out[:, 32 * band + 16 : 32 * band + 32] = im.astype(jnp.bfloat16).reshape(16, 16, 128)
-        for slot in range(BANDS):
-            total = targets[slot, 0] * re + targets[slot, 1] * im
-            same[slot, band] = total.reshape(GRID, 8, 128).sum(0)
-            total = targets[slot, 1] * re - targets[slot, 0] * im
-            cross[slot, band] = total.reshape(GRID, 8, 128).sum(0)
-    keys = [(slot, band) for slot in range(BANDS) for band in range(OWN)]
-    totals = [jnp.sum(group[key], 0, keepdims=True) for group in (same, cross) for key in keys]
-    totals = jnp.sum(jnp.concatenate(totals, 0), 1, keepdims=True)
-    totals = jnp.broadcast_to(totals, (16, 128))
-    lane = lax.broadcasted_iota(jnp.int32, (8, 128), 1)
-    value = jnp.where(lane < 64, totals[:8], totals[8:])
+        for slot, own, cross in PAIRS:
+            if own == band:
+                if cross:
+                    total = targets[slot, 1] * re - targets[slot, 0] * im
+                else:
+                    total = targets[slot, 0] * re + targets[slot, 1] * im
+                sums[slot, own, cross] = total.reshape(GRID, 8, 128).sum(0)
+    value = jnp.concatenate([jnp.sum(sums[key], 0, keepdims=True) for key in PAIRS], 0)
+    value = jnp.broadcast_to(jnp.sum(value, 1, keepdims=True), (8, 128))
+    piece = lax.broadcasted_iota(jnp.int32, (8, 128), 1) // 32
     high = value.astype(jnp.bfloat16).astype(jnp.float32)
     middle = (value - high).astype(jnp.bfloat16).astype(jnp.float32)
     low = value - high - middle
-    piece = lane % 64 // 16
     value = jnp.where(piece == 0, high, jnp.where(piece == 1, middle, jnp.where(piece == 2, low, 0.0)))
     out[:, FIELD_ROWS:] = jnp.broadcast_to(value.astype(jnp.bfloat16)[None], (16, EXTRA, 128))
 
@@ -153,23 +178,22 @@
         for source in range(8 * group + 1, 8 * group + 8):
             total += shares[source].astype(jnp.float32)
         totals.append(total)
-    same, cross = {}, {}
+    value = {}
     for group in range(2):
         values = totals[group][FIELD_ROWS:]
-        values = values + pltpu.roll(values, 112, 1) + pltpu.roll(values, 96, 1)
+        values = values + pltpu.roll(values, 96, 1) + pltpu.roll(values, 64, 1)
         values = values * (1.0 / CELLS)
-        for slot in range(BANDS):
-            for band in range(OWN):
-                at = OWN * slot + band
-                key = (2 * group + slot) % BANDS, 2 * group + band
-                same[key] = jnp.broadcast_to(values[at : at + 1, 0:1], (8, 128))
-                cross[key] = jnp.broadcast_to(values[at : at + 1, 64:65], (8, 128))
+        for at, (slot, own, cross) in enumerate(PAIRS):
+            key = band_of(slot, group), band_of(own, group), cross
+            value[key] = jnp.broadcast_to(values[at : at + 1, 0:1], (8, 128))
 
     def entry(row, column):
         i, j = row % BANDS, column % BANDS
         if row // BANDS == column // BANDS:
-            return -0.5 * (same[i, j] + same[j, i])
-        return None if i == j else 0.5 * (cross[i, j] - cross[j, i])
+            return -(value[i, j, 0] if (i, j, 0) in value else value[j, i, 0])
+        if i == j:
+            return None
+        return value[i, j, 1] if (i, j, 1) in value else -value[j, i, 1]
 
     size = 2 * BANDS
     factor, inverse = {}, {}
@@ -223,15 +247,14 @@
     return jax.ShapeDtypeStruct(shape, dtype)
 
 
-def spread(plane):
-    shape = array(GRID, 4 * PLANE, 128, dtype=jnp.bfloat16)
-    return call(spread_kernel, "spread", shape, [VMEM], [], 1, plane)
-
-
-def prepare(mine, theirs, targets):
-    shapes = (array(2, ROWS, 128), array(BANDS, 2, ROWS, 128))
+def prepare(mine, theirs):
+    return call(coulomb_kernel, "coulomb", array(2, ROWS, 128), [SMEM, SMEM], [], 2, mine, theirs)
+
+
+def apart(place, targets):
     scratch = [pltpu.VMEM((2 * ROWS, 128), jnp.float32)]
-    return call(prepare_kernel, "prepare", shapes, [SMEM, SMEM, VMEM], scratch, 8, mine, theirs, targets)
+    shape = array(BANDS, 2, ROWS, 128)
+    return call(apart_kernel, "apart", shape, [SMEM, VMEM], scratch, 4, place, targets)
 
 
 def exchange(*operands):
@@ -255,11 +278,13 @@
 def local(targets, partners, pair_map, shifts):
     left, right, twist = (jnp.asarray(table) for table in tables())
     place = lax.axis_index("xh")
-    operand = spread(interleaved(partners[0]).reshape(4 * PLANE, 128)).reshape(2 * GRID, 2 * PLANE, 128)
+    plane = interleaved(partners[0]).reshape(1, 4 * PLANE, 128)
+    operand = jnp.broadcast_to(plane, (GRID, 4 * PLANE, 128)).reshape(2 * GRID, 2 * PLANE, 128)
     gathered = lax.all_to_all(operand, ("xh", "ka"), 0, 0, tiled=True)
     mine = jnp.concatenate([pair_map, shifts[0], place.reshape(1, 1)], 1)
     theirs = lax.ppermute(mine, "xh", [(0, 1), (1, 0)])
-    kernel, parts = prepare(mine, theirs, interleaved(targets[0]))
+    parts = apart(place.reshape(1, 1), interleaved(targets[0]))
+    kernel = prepare(mine, theirs)
     gathered, kernel, parts = lax.optimization_barrier((gathered, kernel, parts))
     count = lax.axis_size("ka")
     swapped = lax.ppermute(gathered, "ka", [(i, i ^ 1) for i in range(count)])

time: 56.2 us -> 54.9 us (0.977)
  Pallas kernels: 6.69 us -> 4.81 us
  waiting for transfers between devices: 3.73 us -> 4.72 us
    pallas_call x5, Pallas kernels: 6.69 us -> 4.81 us  [call(): pl.pallas_call(kernel, out_shape=shapes, in_specs=specs, out_specs=jax.tr...]
    unnamed x12 -> x10, local copies, waits for them, and re-layouts: 2.4 us -> 0.67 us
    broadcast_in_dim x0 -> x1, local copies, waits for them, and re-layouts: none -> 1.48 us  [local(): jnp.broadcast_to(plane, (GRID, 4 * PLANE, 128))]
    all_to_all x1, waiting for transfers between devices: 2.49 us -> 3.71 us  [local(): gathered = lax.all_to_all(operand, ('xh', 'ka'), 0, 0, tiled=True)]
  transfers between devices with their start and end apart: 3 -> 3, of which waited for: 2 -> 2; matrix products, arithmetic and copies ran while one was open for 0% -> 0% of each run, Pallas kernels for 5% -> 4%
where the time goes in v3:
time: 54.9 us; the launch traced here: 54.4 us
  blocking collectives  23.1 us (42%)
  starting transfers between devices  18.8 us (34%)
  Pallas kernels  4.81 us (9%)
  waiting for transfers between devices  4.72 us (9%)
  local copies, waits for them, and re-layouts  2.16 us (4%)
  between operations  0.78 us (1%)
    all_to_all x1, blocking collectives, local(): shares = lax.all_to_all(shares, ('xh', 'zz'), 0, 0, tiled=True)  23.1 us
    all_to_all x1, starting transfers between devices, local(): gathered = lax.all_to_all(operand, ('xh', 'ka'), 0, 0, tiled=True)  11.6 us
    ppermute x1, starting transfers between devices, local(): theirs = lax.ppermute(mine, 'xh', [(0, 1), (1, 0)])  4.86 us
    pallas_call x5, Pallas kernels, call(): pl.pallas_call(kernel, out_shape=shapes, in_specs=specs, out_specs=jax.tr...  4.81 us
    all_to_all x1, waiting for transfers between devices, local(): gathered = lax.all_to_all(operand, ('xh', 'ka'), 0, 0, tiled=True)  3.71 us
    ppermute x1, starting transfers between devices, local(): swapped = lax.ppermute(gathered, 'ka', [(i, i ^ 1) for i in range(count)])  2.36 us
    broadcast_in_dim x1, local copies, waits for them, and re-layouts, local(): jnp.broadcast_to(plane, (GRID, 4 * PLANE, 128))  1.48 us
  transfers between devices with their start and end apart: 3, of which 2 were waited for; matrix products, arithmetic and copies ran while one was open for 0% of the time, Pallas kernels for 4%

profile of v3, /device:TPU:1, one launch (start us, length us, event | category | flops | bytes accessed | tf_op | source)
XLA Modules:
  0.0 54.4 jit_solution(8426848613889395859)
XLA Ops:
  0.0 0.0 copy-start.3
  0.0 1.5 %broadcast_in_dim.8 = bf16[32,32,128]{2,1,0:T(8,128)(2,1)} broadcast(bf16[32,128]{1,0:T(8,128)(2,1)} %bitcast.19), dimensions={1,2} | broadcast | bytes 270336 | tf_op jit(solution)/shard_map/broadcast_in_dim | solution.py:282
  1.5 11.6 %all-to-all-start = ((bf16[64,16,128]{2,1,0:T(8,128)(2,1)}), bf16[64,16,128]{2,1,0:T(8,128)(2,1)S(1)}, u32[]{:S(2)}, u32[]{:S(2)}) async-start(bf16[64,16,128]{2,1,0:T(8,128)(2,1)} %bitcast.3), calls=%async_computation | async-start | bytes 524288 | tf_op jit(solution)/shard_map/all_to_all | solution.py:283
  13.8 0.0 copy-start.4
  13.8 0.6 %copy-done.4 = s32[1,1,3]{2,1,0:T(1,128)S(1)} copy-done((s32[1,1,3]{2,1,0:T(1,128)S(1)}, s32[1,1,3]{2,1,0:T(1,128)}, u32[]{:S(2)}) %copy-start.4) | copy-done | bytes 36
  14.4 0.1 pad_add_fusion.mine
  14.5 4.9 %collective-permute-start = (s32[1,5]{1,0:T(1,128)S(1)}, s32[1,5]{1,0:T(1,128)S(1)}, u32[]{:S(2)}, u32[]{:S(2)}) collective-permute-start(s32[1,5]{1,0:T(1,128)S(1)} %pad_add_fusion.mine), channel_id=1, source_target_pairs={{0,8},{8,0},{1,9},{9,1},{2,10},{10,2},{3,11},{11,3},{4,12},{12,4},... | collective-permute-start | bytes 68 | tf_op jit(solution)/shard_map/ppermute | solution.py:285
  19.4 0.0 copy-done.3
  19.4 0.0 copy-start
  19.4 0.0 copy-start.2
  19.4 0.2 apart.1.targets
  19.6 0.0 copy-start.1
  19.6 1.0 %collective-permute-done.theirs = s32[1,5]{1,0:T(1,128)S(1)} collective-permute-done((s32[1,5]{1,0:T(1,128)S(1)}, s32[1,5]{1,0:T(1,128)S(1)}, u32[]{:S(2)}, u32[]{:S(2)}) %collective-permute-start) | collective-permute-done | bytes 52 | tf_op jit(solution)/shard_map/ppermute | solution.py:285
  20.6 0.8 %coulomb.1.kernel = f32[2,256,128]{2,1,0:T(8,128)S(1)} custom-call(s32[1,5]{1,0:T(1,128)S(1)} %pad_add_fusion.mine, s32[1,5]{1,0:T(1,128)S(1)} %collective-permute-done.theirs), custom_call_target="tpu_custom_call" | custom-call | tf_op jit(solution)/shard_map/coulomb/pallas_call | solution.py:235
  21.4 3.7 %all-to-all-done.gathered = bf16[64,16,128]{2,1,0:T(8,128)(2,1)S(1)} async-done(((bf16[64,16,128]{2,1,0:T(8,128)(2,1)}), bf16[64,16,128]{2,1,0:T(8,128)(2,1)S(1)}, u32[]{:S(2)}, u32[]{:S(2)}) %all-to-all-start) | async-done | bytes 262176 | tf_op jit(solution)/shard_map/all_to_all | solution.py:283
  25.1 2.4 %collective-permute-start.1 = (bf16[64,16,128]{2,1,0:T(8,128)(2,1)S(1)}, bf16[64,16,128]{2,1,0:T(8,128)(2,1)S(1)}, u32[]{:S(2)}, u32[]{:S(2)}) collective-permute-start(bf16[64,16,128]{2,1,0:T(8,128)(2,1)S(1)} %all-to-all-done.gathered), channel_id=1, source_target_pairs={{0,16},{16,0},{32,48},{48,32},{64,80},{80,64},{96,112},{112,96},{1... | collective-permute-start | bytes 786440 | tf_op jit(solution)/shard_map/ppermute | solution.py:290
  27.4 0.0 copy-done
  27.4 0.0 copy-done.2
  27.5 0.0 copy-done.1
  27.5 1.4 %first.1.before = f32[2,2,256,128]{3,2,1,0:T(8,128)S(1)} custom-call(f32[2,256,128]{2,1,0:T(8,128)S(1)} %coulomb.1.kernel, f32[4,2,256,128]{3,2,1,0:T(8,128)S(1)} %apart.1.targets, bf16[64,16,128]{2,1,0:T(8,128)(2,1)S(1)} %all-to-all-done.gathered, bf16[512,512]{1,0:T(8,128)(2,1)S(1)} %copy-done, bf16[256,256]{1,0:T(8,128)(2,1)S(1)} %copy-done.2, ...), custom_call_target="tpu_custom_call" | custom-call | tf_op jit(solution)/shard_map/first/pallas_call | solution.py:235
  28.8 0.0 collective-permute-done.1.gathered
  28.8 1.6 %second.1 = bf16[16,72,128]{2,1,0:T(8,128)(2,1)S(1)} custom-call(f32[2,256,128]{2,1,0:T(8,128)S(1)} %coulomb.1.kernel, f32[4,2,256,128]{3,2,1,0:T(8,128)S(1)} %apart.1.targets, bf16[64,16,128]{2,1,0:T(8,128)(2,1)S(1)} %collective-permute-done.1.gathered, bf16[512,512]{1,0:T(8,128)(2,1)S(1)} %copy-done, bf16[256,256]{1,0:T(8,128)(2,1)S(1)} %copy-done.2, ...), custom_call_target="tpu_custom_call" | custom-call | tf_op jit(solution)/shard_map/second/pallas_call | solution.py:235
  30.5 23.1 %all_to_all.10.shares = bf16[16,72,128]{2,1,0:T(8,128)(2,1)S(1)} all-to-all(bf16[16,72,128]{2,1,0:T(8,128)(2,1)S(1)} %second.1), channel_id=1, replica_groups=mesh['ka'=32,'xh'=2,'zz'=8] {'xh','zz'}, dimensions={0} | all-to-all | bytes 589824 | tf_op jit(solution)/shard_map/all_to_all | solution.py:293
  53.6 0.9 %projector.1 = f32[256,128]{1,0:T(8,128)} custom-call(bf16[16,72,128]{2,1,0:T(8,128)(2,1)S(1)} %all_to_all.10.shares), custom_call_target="tpu_custom_call" | custom-call | tf_op jit(solution)/shard_map/projector/pallas_call | solution.py:235
Async XLA Ops:
  0.0 19.4 %copy-start.3 = (bf16[1,4,2,32768]{3,2,1,0:T(2,128)(2,1)S(1)}, bf16[1,4,2,32768]{3,2,1,0:T(2,128)(2,1)}, u32[]{:S(2)}) copy-start(bf16[1,4,2,32768]{3,2,1,0:T(2,128)(2,1)} %param.7) | copy-start | bytes 1572868
  1.5 23.6 %all-to-all-start = ((bf16[64,16,128]{2,1,0:T(8,128)(2,1)}), bf16[64,16,128]{2,1,0:T(8,128)(2,1)S(1)}, u32[]{:S(2)}, u32[]{:S(2)}) async-start(bf16[64,16,128]{2,1,0:T(8,128)(2,1)} %bitcast.3), calls=%async_computation | async-start | bytes 524288 | tf_op jit(solution)/shard_map/all_to_all | solution.py:283
  13.8 0.7 %copy-start.4 = (s32[1,1,3]{2,1,0:T(1,128)S(1)}, s32[1,1,3]{2,1,0:T(1,128)}, u32[]{:S(2)}) copy-start(s32[1,1,3]{2,1,0:T(1,128)} %param.10) | copy-start | bytes 40
  14.5 6.1 %collective-permute-start = (s32[1,5]{1,0:T(1,128)S(1)}, s32[1,5]{1,0:T(1,128)S(1)}, u32[]{:S(2)}, u32[]{:S(2)}) collective-permute-start(s32[1,5]{1,0:T(1,128)S(1)} %pad_add_fusion.mine), channel_id=1, source_target_pairs={{0,8},{8,0},{1,9},{9,1},{2,10},{10,2},{3,11},{11,3},{4,12},{12,4},... | collective-permute-start | bytes 68 | tf_op jit(solution)/shard_map/ppermute | solution.py:285
  19.4 8.1 %copy-start = (bf16[512,512]{1,0:T(8,128)(2,1)S(1)}, bf16[512,512]{1,0:T(8,128)(2,1)}, u32[]{:S(2)}) copy-start(bf16[512,512]{1,0:T(8,128)(2,1)} %constant.12.clone.left) | copy-start | bytes 1572868
  19.4 8.1 %copy-start.2 = (bf16[256,256]{1,0:T(8,128)(2,1)S(1)}, bf16[256,256]{1,0:T(8,128)(2,1)}, u32[]{:S(2)}) copy-start(bf16[256,256]{1,0:T(8,128)(2,1)} %constant.13.clone.right) | copy-start | bytes 393220
  19.6 7.9 %copy-start.1 = (f32[2,256,128]{2,1,0:T(8,128)S(1)}, f32[2,256,128]{2,1,0:T(8,128)}, u32[]{:S(2)}) copy-start(f32[2,256,128]{2,1,0:T(8,128)} %constant.14.clone.twist) | copy-start | bytes 786436
  25.1 3.8 %collective-permute-start.1 = (bf16[64,16,128]{2,1,0:T(8,128)(2,1)S(1)}, bf16[64,16,128]{2,1,0:T(8,128)(2,1)S(1)}, u32[]{:S(2)}, u32[]{:S(2)}) collective-permute-start(bf16[64,16,128]{2,1,0:T(8,128)(2,1)S(1)} %all-to-all-done.gathered), channel_id=1, source_target_pairs={{0,16},{16,0},{32,48},{48,32},{64,80},{80,64},{96,112},{112,96},{1... | collective-permute-start | bytes 786440 | tf_op jit(solution)/shard_map/ppermute | solution.py:290

commit v4 on v3

--- a/solution.py
+++ b/solution.py
@@ -9,6 +9,7 @@
 
 GRID = 32
 BANDS = 4
+OCC = 2
 OWN = 2
 PLANE = 8
 ROWS = GRID * PLANE
@@ -17,6 +18,8 @@
 SCREENING_CUTOFF = 0.25
 FIELD_ROWS = 32 * OWN
 EXTRA = 8
+PEERS = 32
+NUMBERS = 8
 PAIRS = [(0, 0, 0), (1, 1, 0), (0, 1, 0), (0, 1, 1), (2, 0, 0), (2, 0, 1), (3, 1, 0), (3, 1, 1)]
 
 
@@ -59,11 +62,33 @@
     return jnp.dot(a, b, preferred_element_type=jnp.float32)
 
 
-def coulomb_kernel(mine, theirs, kernel):
-    place = mine[0, 4]
+def spread_kernel(plane, offset, shift, out, tile, shift_now, arrive, leave):
+    copies = [
+        pltpu.make_async_copy(shift, shift_now, arrive.at[0]),
+        pltpu.make_async_copy(plane, tile.at[0 : 4 * PLANE], arrive.at[1]),
+    ]
+    for copy in copies:
+        copy.start()
+    copies[0].wait()
+    row = lax.broadcasted_iota(jnp.int32, (NUMBERS, 128), 0)
+    value = jnp.zeros((NUMBERS, 128), jnp.int32) + offset[0, 0]
+    for axis in range(3):
+        value = jnp.where(row == axis + 1, shift_now[0, axis], value)
+    tile[4 * PLANE :] = value.astype(jnp.float32).astype(jnp.bfloat16)
+    copies[1].wait()
+    copies = [pltpu.make_async_copy(tile, out.at[at], leave.at[at]) for at in range(PEERS)]
+    for copy in copies:
+        copy.start()
+    for copy in copies:
+        copy.wait()
+
+
+def coulomb_kernel(place, gathered, kernel):
     for q in range(2):
-        number = [jnp.where(place == q, mine[0, at], theirs[0, at]) for at in range(4)]
-        kernel[q] = coulomb(number[0], number[1:]) * (1.0 / CELLS)
+        numbers = gathered[place[0, 0] + q * (PEERS // 2), 4 * PLANE :].astype(jnp.float32)
+        numbers = numbers.astype(jnp.int32)
+        shift = [numbers[axis + 1 : axis + 2] for axis in range(3)]
+        kernel[q] = coulomb(numbers[0:1], shift) * (1.0 / CELLS)
 
 
 def apart_kernel(place, targets, parts, rows):
@@ -77,20 +102,26 @@
     return 2 * place + slot if slot < OWN else slot - (1 + 2 * (slot - OWN)) * place
 
 
-def fields_of(kernel, targets, gathered, left, right, twist, rows, parts):
-    rows[...] = gathered[...].astype(jnp.float32).reshape(4 * ROWS, 128)
+def exchange_kernel(core, kernel, targets, own, other, left, right, twist, out, rows, parts):
+    for source, parity in ((own, core[0, 0]), (other, 1 - core[0, 0])):
+        for q in range(2):
+            for j in range(OCC):
+                planes = source[16 * q : 16 * q + 16, 16 * j : 16 * j + 16].astype(jnp.float32)
+                rows[q, j, :, pl.ds(parity, 1)] = planes[:, None]
     for q in range(2):
-        for part in range(2):
-            parts[q, part] = rows[pl.ds(2 * ROWS * q + part, ROWS, 2), :]
+        for j in range(OCC):
+            for part in range(2):
+                parts[j, q, part] = rows[q, j, :, :, pl.ds(part, PLANE, 2), :].reshape(ROWS, 128)
 
     def twisted(re, im):
         return re * twist[0] + im * twist[1], im * twist[0] - re * twist[1]
 
-    def density(band):
+    def density(band, j):
         tops, bottoms = [], []
         for q in range(2):
-            tops.append(parts[q, 0] * targets[band, 0] + parts[q, 1] * targets[band, 1])
-            bottoms.append(parts[q, 0] * targets[band, 1] - parts[q, 1] * targets[band, 0])
+            re, im = parts[j, q, 0], parts[j, q, 1]
+            tops.append(re * targets[band, 0] + im * targets[band, 1])
+            bottoms.append(re * targets[band, 1] - im * targets[band, 0])
         return joined(tops, bottoms)
 
     def joined(tops, bottoms):
@@ -122,45 +153,35 @@
             bottoms.append(im)
         return joined(tops, bottoms)
 
-    def field(conjugate):
+    def field(conjugates):
         re_sum, im_sum = None, None
-        for q in range(2):
-            cut = slice(128 * q, 128 * q + 128)
-            re, im = conjugate[:ROWS, cut], conjugate[ROWS:, cut]
-            re_now = -(parts[q, 0] * re) - parts[q, 1] * im
-            im_now = parts[q, 0] * im - parts[q, 1] * re
-            re_sum = re_now if re_sum is None else re_sum + re_now
-            im_sum = im_now if im_sum is None else im_sum + im_now
+        for j in range(OCC):
+            for q in range(2):
+                cut = slice(128 * q, 128 * q + 128)
+                re, im = conjugates[j][:ROWS, cut], conjugates[j][ROWS:, cut]
+                re_now = -(parts[j, q, 0] * re) - parts[j, q, 1] * im
+                im_now = parts[j, q, 0] * im - parts[j, q, 1] * re
+                re_sum = re_now if re_sum is None else re_sum + re_now
+                im_sum = im_now if im_sum is None else im_sum + im_now
         return re_sum, im_sum
 
-    values = [product(left[...], density(band)) for band in range(OWN)]
+    units = [(band, j) for band in range(OWN) for j in range(OCC)]
+    values = [product(left[...], density(*unit)) for unit in units]
     values = [to_spectrum(value) for value in values]
     values = [from_spectrum(value) for value in values]
     values = [product(left[...], untwisted(value)) for value in values]
-    for band, value in enumerate(values):
-        yield (band, *field(value))
-
-
-def first_kernel(kernel, targets, gathered, left, right, twist, out, rows, parts):
-    for band, re, im in fields_of(kernel, targets, gathered, left, right, twist, rows, parts):
-        out[band, 0] = re
-        out[band, 1] = im
-
-
-def second_kernel(kernel, targets, gathered, left, right, twist, before, out, rows, parts):
     sums = {}
-    for band, re, im in fields_of(kernel, targets, gathered, left, right, twist, rows, parts):
-        re += before[band, 0]
-        im += before[band, 1]
+    for band in range(OWN):
+        re, im = field(values[OCC * band : OCC * band + OCC])
         out[:, 32 * band : 32 * band + 16] = re.astype(jnp.bfloat16).reshape(16, 16, 128)
         out[:, 32 * band + 16 : 32 * band + 32] = im.astype(jnp.bfloat16).reshape(16, 16, 128)
-        for slot, own, cross in PAIRS:
-            if own == band:
+        for slot, place, cross in PAIRS:
+            if place == band:
                 if cross:
                     total = targets[slot, 1] * re - targets[slot, 0] * im
                 else:
                     total = targets[slot, 0] * re + targets[slot, 1] * im
-                sums[slot, own, cross] = total.reshape(GRID, 8, 128).sum(0)
+                sums[slot, place, cross] = total.reshape(GRID, 8, 128).sum(0)
     value = jnp.concatenate([jnp.sum(sums[key], 0, keepdims=True) for key in PAIRS], 0)
     value = jnp.broadcast_to(jnp.sum(value, 1, keepdims=True), (8, 128))
     piece = lax.broadcasted_iota(jnp.int32, (8, 128), 1) // 32
@@ -247,8 +268,32 @@
     return jax.ShapeDtypeStruct(shape, dtype)
 
 
-def prepare(mine, theirs):
-    return call(coulomb_kernel, "coulomb", array(2, ROWS, 128), [SMEM, SMEM], [], 2, mine, theirs)
+def stay(operand):
+    return pltpu.with_memory_space_constraint(operand, pltpu.HBM)
+
+
+def spread(plane, offset, shift):
+    rows = 4 * PLANE + NUMBERS
+    scratch = [
+        pltpu.VMEM((rows, 128), jnp.bfloat16),
+        pltpu.SMEM((1, 3), jnp.int32),
+        pltpu.SemaphoreType.DMA((2,)),
+        pltpu.SemaphoreType.DMA((PEERS,)),
+    ]
+    hbm = pl.BlockSpec(memory_space=pltpu.HBM)
+    return pl.pallas_call(
+        spread_kernel,
+        out_shape=array(PEERS, rows, 128, dtype=jnp.bfloat16),
+        in_specs=[hbm, SMEM, hbm],
+        out_specs=hbm,
+        scratch_shapes=scratch,
+        compiler_params=pltpu.CompilerParams(vmem_limit_bytes=1 << 20),
+        name="spread",
+    )(stay(plane), offset, stay(shift))
+
+
+def prepare(place, gathered):
+    return call(coulomb_kernel, "coulomb", array(2, ROWS, 128), [SMEM, VMEM], [], 2, place, gathered)
 
 
 def apart(place, targets):
@@ -258,12 +303,13 @@
 
 
 def exchange(*operands):
-    scratch = [pltpu.VMEM((4 * ROWS, 128), jnp.float32), pltpu.VMEM((2, 2, ROWS, 128), jnp.float32)]
-    specs = [VMEM] * len(operands)
-    if len(operands) == 6:
-        return call(first_kernel, "first", array(OWN, 2, ROWS, 128), specs, scratch, 16, *operands)
+    scratch = [
+        pltpu.VMEM((2, OCC, GRID // 2, 2, 2 * PLANE, 128), jnp.float32),
+        pltpu.VMEM((OCC, 2, 2, ROWS, 128), jnp.float32),
+    ]
     shape = array(16, FIELD_ROWS + EXTRA, 128, dtype=jnp.bfloat16)
-    return call(second_kernel, "second", shape, specs, scratch, 16, *operands)
+    specs = [SMEM] + [VMEM] * (len(operands) - 1)
+    return call(exchange_kernel, "exchange", shape, specs, scratch, 24, *operands)
 
 
 def projector(shares):
@@ -277,35 +323,32 @@
 
 def local(targets, partners, pair_map, shifts):
     left, right, twist = (jnp.asarray(table) for table in tables())
-    place = lax.axis_index("xh")
-    plane = interleaved(partners[0]).reshape(1, 4 * PLANE, 128)
-    operand = jnp.broadcast_to(plane, (GRID, 4 * PLANE, 128)).reshape(2 * GRID, 2 * PLANE, 128)
-    gathered = lax.all_to_all(operand, ("xh", "ka"), 0, 0, tiled=True)
-    mine = jnp.concatenate([pair_map, shifts[0], place.reshape(1, 1)], 1)
-    theirs = lax.ppermute(mine, "xh", [(0, 1), (1, 0)])
-    parts = apart(place.reshape(1, 1), interleaved(targets[0]))
-    kernel = prepare(mine, theirs)
-    gathered, kernel, parts = lax.optimization_barrier((gathered, kernel, parts))
-    count = lax.axis_size("ka")
-    swapped = lax.ppermute(gathered, "ka", [(i, i ^ 1) for i in range(count)])
-    before = exchange(kernel, parts, gathered, left, right, twist)
-    shares = exchange(kernel, parts, swapped, left, right, twist, before)
+    place, core, group = (lax.axis_index(axis).reshape(1, 1) for axis in ("chip", "core", "xh"))
+    plane = interleaved(partners[0]).reshape(4 * PLANE, 128)
+    operand = spread(plane, pair_map, shifts[0])
+    gathered = lax.all_to_all(operand, ("xh", "chip"), 0, 0, tiled=True)
+    parts = apart(group, interleaved(targets[0]))
+    gathered, parts = lax.optimization_barrier((gathered, parts))
+    swapped = lax.ppermute(gathered, "core", [(0, 1), (1, 0)])
+    kernel = prepare(place, gathered)
+    shares = exchange(core, kernel, parts, gathered, swapped, left, right, twist)
     shares = lax.all_to_all(shares, ("xh", "zz"), 0, 0, tiled=True)
     rows = projector(shares).reshape(2 * BANDS, 16, 2, 128)
     return jnp.swapaxes(rows, 1, 2).reshape(1, 2 * BANDS, 2, 2048)
 
 
 def solution(mesh):
-    split = Mesh(mesh.devices.reshape(GRID, 2, 8), ("ka", "xh", "zz"))
+    split = Mesh(mesh.devices.reshape(16, 2, 2, 8), ("chip", "core", "xh", "zz"))
+    ka, pb = ("chip", "core"), ("xh", "zz")
     return jax.shard_map(
         local,
         mesh=split,
         in_specs=(
-            P("ka", None, None, None),
-            P(("xh", "zz"), None, None, "ka"),
-            P("ka", ("xh", "zz")),
-            P("ka", ("xh", "zz"), None),
+            P(ka, None, None, None),
+            P(pb, None, None, ka),
+            P(ka, pb),
+            P(ka, pb, None),
         ),
-        out_specs=P("ka", None, None, ("xh", "zz")),
+        out_specs=P(ka, None, None, pb),
         check_vma=False,
     )

time: 54.9 us -> 57 us (1.038); the launches traced: 54.4 us -> 55.9 us
  waiting for transfers between devices: 4.72 us -> 11 us
  local copies, waits for them, and re-layouts: 2.16 us -> 0.02 us
  starting transfers between devices: 18.8 us -> 16.7 us
  blocking collectives: 23.1 us -> 21.9 us
  Pallas kernels: 4.81 us -> 5.49 us
    all_to_all x1, waiting for transfers between devices: 3.71 us -> 9.97 us  [local(): gathered = lax.all_to_all(operand, ('xh', 'chip'), 0, 0, tiled=True)]
    pallas_call x0 -> x1, Pallas kernels: none -> 1.75 us  [spread(): pl.pallas_call(spread_kernel, out_shape=array(PEERS, rows, 128, dtype=jnp...]
    broadcast_in_dim x1 -> x0, local copies, waits for them, and re-layouts: 1.48 us -> none  [local(): jnp.broadcast_to(plane, (GRID, 4 * PLANE, 128))]
    all_to_all x1, blocking collectives: 23.1 us -> 21.9 us  [local(): shares = lax.all_to_all(shares, ('xh', 'zz'), 0, 0, tiled=True)]
    all_to_all x1, starting transfers between devices: 11.6 us -> 10.5 us  [local(): gathered = lax.all_to_all(operand, ('xh', 'chip'), 0, 0, tiled=True)]
    pallas_call x5 -> x4, Pallas kernels: 4.81 us -> 3.74 us  [call(): pl.pallas_call(kernel, out_shape=shapes, in_specs=specs, out_specs=jax.tr...]
    ppermute x2 -> x1, starting transfers between devices: 7.22 us -> 6.18 us  [local(): swapped = lax.ppermute(gathered, 'core', [(0, 1), (1, 0)])]
    unnamed x10 -> x8, local copies, waits for them, and re-layouts: 0.67 us -> 0.02 us
  transfers between devices with their start and end apart: 3 -> 2, of which waited for: 2 -> 2; matrix products, arithmetic and copies ran while one was open for 0% -> 0% of each run, Pallas kernels for 4% -> 1%
where the time goes in v4:
time: 57 us; the launch traced here: 55.9 us
  blocking collectives  21.9 us (38%)
  starting transfers between devices  16.7 us (29%)
  waiting for transfers between devices  11 us (19%)
  Pallas kernels  5.49 us (10%)
  between operations  0.8 us (1%)
    all_to_all x1, blocking collectives, local(): shares = lax.all_to_all(shares, ('xh', 'zz'), 0, 0, tiled=True)  21.9 us
    all_to_all x1, starting transfers between devices, local(): gathered = lax.all_to_all(operand, ('xh', 'chip'), 0, 0, tiled=True)  10.5 us
    all_to_all x1, waiting for transfers between devices, local(): gathered = lax.all_to_all(operand, ('xh', 'chip'), 0, 0, tiled=True)  9.97 us
    ppermute x1, starting transfers between devices, local(): swapped = lax.ppermute(gathered, 'core', [(0, 1), (1, 0)])  6.18 us
    pallas_call x4, Pallas kernels, call(): pl.pallas_call(kernel, out_shape=shapes, in_specs=specs, out_specs=jax.tr...  3.74 us
    pallas_call x1, Pallas kernels, spread(): pl.pallas_call(spread_kernel, out_shape=array(PEERS, rows, 128, dtype=jnp...  1.75 us
  transfers between devices with their start and end apart: 2, of which 2 were waited for; matrix products, arithmetic and copies ran while one was open for 0% of the time, Pallas kernels for 1%

profile of v4, /device:TPU:1, one launch (start us, length us, event | category | flops | bytes accessed | tf_op | source)
XLA Modules:
  0.0 55.9 jit_solution(16292114503994541500)
XLA Ops:
  0.0 0.0 copy-start
  0.7 1.7 %spread.1 = bf16[32,40,128]{2,1,0:T(8,128)(2,1)} custom-call(bf16[32,128]{1,0:T(8,128)(2,1)} %bitcast.20, s32[1,1]{1,0:T(1,128)S(6)} %copy.11.offset, s32[1,3]{1,0:T(1,128)} %bitcast.21), custom_call_target="tpu_custom_call" | custom-call | tf_op jit(solution)/shard_map/spread/pallas_call | solution.py:284
  2.5 10.5 %all-to-all-start = ((bf16[32,40,128]{2,1,0:T(8,128)(2,1)}), bf16[32,40,128]{2,1,0:T(8,128)(2,1)S(1)}, u32[]{:S(2)}, u32[]{:S(2)}) async-start(bf16[32,40,128]{2,1,0:T(8,128)(2,1)} %spread.1), calls=%async_computation | async-start | bytes 655360 | tf_op jit(solution)/shard_map/all_to_all | solution.py:329
  13.0 0.0 copy-done
  13.0 0.0 copy-start.2
  13.0 0.0 copy-start.3
  13.0 0.2 apart.1.targets
  13.2 0.0 copy-start.1
  13.2 10.0 %all-to-all-done.gathered.own = bf16[32,40,128]{2,1,0:T(8,128)(2,1)S(1)} async-done(((bf16[32,40,128]{2,1,0:T(8,128)(2,1)}), bf16[32,40,128]{2,1,0:T(8,128)(2,1)S(1)}, u32[]{:S(2)}, u32[]{:S(2)}) %all-to-all-start) | async-done | bytes 327712 | tf_op jit(solution)/shard_map/all_to_all | solution.py:329
  23.2 6.2 %collective-permute-start = (bf16[32,40,128]{2,1,0:T(8,128)(2,1)S(1)}, bf16[32,40,128]{2,1,0:T(8,128)(2,1)S(1)}, u32[]{:S(2)}, u32[]{:S(2)}) collective-permute-start(bf16[32,40,128]{2,1,0:T(8,128)(2,1)S(1)} %all-to-all-done.gathered.own), channel_id=1, source_target_pairs={{0,16},{16,0},{1,17},{17,1},{2,18},{18,2},{3,19},{19,3},{4,20},{20... | collective-permute-start | bytes 983048 | tf_op jit(solution)/shard_map/ppermute | solution.py:332
  29.4 0.2 coulomb.1.kernel
  29.6 1.0 %collective-permute-done.other = bf16[32,40,128]{2,1,0:T(8,128)(2,1)S(1)} collective-permute-done((bf16[32,40,128]{2,1,0:T(8,128)(2,1)S(1)}, bf16[32,40,128]{2,1,0:T(8,128)(2,1)S(1)}, u32[]{:S(2)}, u32[]{:S(2)}) %collective-permute-start) | collective-permute-done | bytes 327712 | tf_op jit(solution)/shard_map/ppermute | solution.py:332
  30.6 0.0 copy-done.2
  30.6 0.0 copy-done.3
  30.6 0.0 copy-done.1
  30.6 2.5 %exchange.1 = bf16[16,72,128]{2,1,0:T(8,128)(2,1)S(1)} custom-call(s32[1,1]{1,0:T(1,128)} %bitcast.core, f32[2,256,128]{2,1,0:T(8,128)S(1)} %coulomb.1.kernel, f32[4,2,256,128]{3,2,1,0:T(8,128)S(1)} %apart.1.targets, bf16[32,40,128]{2,1,0:T(8,128)(2,1)S(1)} %all-to-all-done.gathered.own, bf16[32,40,128]{2,1,0:T(8,128)(2,1)S(1)} %collective-permute-done.other, ...), custom_call_target="tpu_custom_call" | custom-call | tf_op jit(solution)/shard_map/exchange/pallas_call | solution.py:256
  33.1 21.9 %all_to_all.10.shares = bf16[16,72,128]{2,1,0:T(8,128)(2,1)S(1)} all-to-all(bf16[16,72,128]{2,1,0:T(8,128)(2,1)S(1)} %exchange.1), channel_id=1, replica_groups=mesh['chip'=16,'core'=2,'xh'=2,'zz'=8] {'xh','zz'}, dimensions={0} | all-to-all | bytes 589824 | tf_op jit(solution)/shard_map/all_to_all | solution.py:335
  55.0 0.9 %projector.1 = f32[256,128]{1,0:T(8,128)} custom-call(bf16[16,72,128]{2,1,0:T(8,128)(2,1)S(1)} %all_to_all.10.shares), custom_call_target="tpu_custom_call" | custom-call | tf_op jit(solution)/shard_map/projector/pallas_call | solution.py:256
Async XLA Ops:
  0.0 13.0 %copy-start = (bf16[1,4,2,32768]{3,2,1,0:T(2,128)(2,1)S(1)}, bf16[1,4,2,32768]{3,2,1,0:T(2,128)(2,1)}, u32[]{:S(2)}) copy-start(bf16[1,4,2,32768]{3,2,1,0:T(2,128)(2,1)} %param.7) | copy-start | bytes 1572868
  2.5 20.7 %all-to-all-start = ((bf16[32,40,128]{2,1,0:T(8,128)(2,1)}), bf16[32,40,128]{2,1,0:T(8,128)(2,1)S(1)}, u32[]{:S(2)}, u32[]{:S(2)}) async-start(bf16[32,40,128]{2,1,0:T(8,128)(2,1)} %spread.1), calls=%async_computation | async-start | bytes 655360 | tf_op jit(solution)/shard_map/all_to_all | solution.py:329
  13.0 17.6 %copy-start.2 = (f32[2,256,128]{2,1,0:T(8,128)S(1)}, f32[2,256,128]{2,1,0:T(8,128)}, u32[]{:S(2)}) copy-start(f32[2,256,128]{2,1,0:T(8,128)} %constant.23.clone.twist) | copy-start | bytes 786436
  13.0 17.6 %copy-start.3 = (bf16[256,256]{1,0:T(8,128)(2,1)S(1)}, bf16[256,256]{1,0:T(8,128)(2,1)}, u32[]{:S(2)}) copy-start(bf16[256,256]{1,0:T(8,128)(2,1)} %constant.22.clone.right) | copy-start | bytes 393220
  13.2 17.4 %copy-start.1 = (bf16[512,512]{1,0:T(8,128)(2,1)S(1)}, bf16[512,512]{1,0:T(8,128)(2,1)}, u32[]{:S(2)}) copy-start(bf16[512,512]{1,0:T(8,128)(2,1)} %constant.21.clone.left) | copy-start | bytes 1572868
  23.2 7.4 %collective-permute-start = (bf16[32,40,128]{2,1,0:T(8,128)(2,1)S(1)}, bf16[32,40,128]{2,1,0:T(8,128)(2,1)S(1)}, u32[]{:S(2)}, u32[]{:S(2)}) collective-permute-start(bf16[32,40,128]{2,1,0:T(8,128)(2,1)S(1)} %all-to-all-done.gathered.own), channel_id=1, source_target_pairs={{0,16},{16,0},{1,17},{17,1},{2,18},{18,2},{3,19},{19,3},{4,20},{20... | collective-permute-start | bytes 983048 | tf_op jit(solution)/shard_map/ppermute | solution.py:332

commit v5 on v4

--- a/solution.py
+++ b/solution.py
@@ -19,7 +19,6 @@
 FIELD_ROWS = 32 * OWN
 EXTRA = 8
 PEERS = 32
-NUMBERS = 8
 PAIRS = [(0, 0, 0), (1, 1, 0), (0, 1, 0), (0, 1, 1), (2, 0, 0), (2, 0, 1), (3, 1, 0), (3, 1, 1)]
 
 
@@ -62,33 +61,11 @@
     return jnp.dot(a, b, preferred_element_type=jnp.float32)
 
 
-def spread_kernel(plane, offset, shift, out, tile, shift_now, arrive, leave):
-    copies = [
-        pltpu.make_async_copy(shift, shift_now, arrive.at[0]),
-        pltpu.make_async_copy(plane, tile.at[0 : 4 * PLANE], arrive.at[1]),
-    ]
-    for copy in copies:
-        copy.start()
-    copies[0].wait()
-    row = lax.broadcasted_iota(jnp.int32, (NUMBERS, 128), 0)
-    value = jnp.zeros((NUMBERS, 128), jnp.int32) + offset[0, 0]
-    for axis in range(3):
-        value = jnp.where(row == axis + 1, shift_now[0, axis], value)
-    tile[4 * PLANE :] = value.astype(jnp.float32).astype(jnp.bfloat16)
-    copies[1].wait()
-    copies = [pltpu.make_async_copy(tile, out.at[at], leave.at[at]) for at in range(PEERS)]
-    for copy in copies:
-        copy.start()
-    for copy in copies:
-        copy.wait()
-
-
-def coulomb_kernel(place, gathered, kernel):
+def coulomb_kernel(mine, theirs, kernel):
+    place = mine[0, 4]
     for q in range(2):
-        numbers = gathered[place[0, 0] + q * (PEERS // 2), 4 * PLANE :].astype(jnp.float32)
-        numbers = numbers.astype(jnp.int32)
-        shift = [numbers[axis + 1 : axis + 2] for axis in range(3)]
-        kernel[q] = coulomb(numbers[0:1], shift) * (1.0 / CELLS)
+        number = [jnp.where(place == q, mine[0, at], theirs[0, at]) for at in range(4)]
+        kernel[q] = coulomb(number[0], number[1:]) * (1.0 / CELLS)
 
 
 def apart_kernel(place, targets, parts, rows):
@@ -268,32 +245,8 @@
     return jax.ShapeDtypeStruct(shape, dtype)
 
 
-def stay(operand):
-    return pltpu.with_memory_space_constraint(operand, pltpu.HBM)
-
-
-def spread(plane, offset, shift):
-    rows = 4 * PLANE + NUMBERS
-    scratch = [
-        pltpu.VMEM((rows, 128), jnp.bfloat16),
-        pltpu.SMEM((1, 3), jnp.int32),
-        pltpu.SemaphoreType.DMA((2,)),
-        pltpu.SemaphoreType.DMA((PEERS,)),
-    ]
-    hbm = pl.BlockSpec(memory_space=pltpu.HBM)
-    return pl.pallas_call(
-        spread_kernel,
-        out_shape=array(PEERS, rows, 128, dtype=jnp.bfloat16),
-        in_specs=[hbm, SMEM, hbm],
-        out_specs=hbm,
-        scratch_shapes=scratch,
-        compiler_params=pltpu.CompilerParams(vmem_limit_bytes=1 << 20),
-        name="spread",
-    )(stay(plane), offset, stay(shift))
-
-
-def prepare(place, gathered):
-    return call(coulomb_kernel, "coulomb", array(2, ROWS, 128), [SMEM, VMEM], [], 2, place, gathered)
+def prepare(mine, theirs):
+    return call(coulomb_kernel, "coulomb", array(2, ROWS, 128), [SMEM, SMEM], [], 2, mine, theirs)
 
 
 def apart(place, targets):
@@ -323,14 +276,16 @@
 
 def local(targets, partners, pair_map, shifts):
     left, right, twist = (jnp.asarray(table) for table in tables())
-    place, core, group = (lax.axis_index(axis).reshape(1, 1) for axis in ("chip", "core", "xh"))
-    plane = interleaved(partners[0]).reshape(4 * PLANE, 128)
-    operand = spread(plane, pair_map, shifts[0])
+    core, group = (lax.axis_index(axis).reshape(1, 1) for axis in ("core", "xh"))
+    plane = interleaved(partners[0]).reshape(1, 4 * PLANE, 128)
+    operand = jnp.broadcast_to(plane, (PEERS, 4 * PLANE, 128))
     gathered = lax.all_to_all(operand, ("xh", "chip"), 0, 0, tiled=True)
+    mine = jnp.concatenate([pair_map, shifts[0], group], 1)
+    theirs = lax.ppermute(mine, "xh", [(0, 1), (1, 0)])
     parts = apart(group, interleaved(targets[0]))
-    gathered, parts = lax.optimization_barrier((gathered, parts))
+    gathered, parts, theirs = lax.optimization_barrier((gathered, parts, theirs))
     swapped = lax.ppermute(gathered, "core", [(0, 1), (1, 0)])
-    kernel = prepare(place, gathered)
+    kernel = prepare(mine, theirs)
     shares = exchange(core, kernel, parts, gathered, swapped, left, right, twist)
     shares = lax.all_to_all(shares, ("xh", "zz"), 0, 0, tiled=True)
     rows = projector(shares).reshape(2 * BANDS, 16, 2, 128)

time: 57 us -> 54.6 us (0.958)
  waiting for transfers between devices: 11 us -> 3.78 us
  starting transfers between devices: 16.7 us -> 20.7 us
  local copies, waits for them, and re-layouts: 0.02 us -> 2.18 us
  Pallas kernels: 5.49 us -> 4.26 us
    all_to_all x1, waiting for transfers between devices: 9.97 us -> 2.19 us  [local(): gathered = lax.all_to_all(operand, ('xh', 'chip'), 0, 0, tiled=True)]
    ppermute x0 -> x1, starting transfers between devices: none -> 4.64 us  [local(): theirs = lax.ppermute(mine, 'xh', [(0, 1), (1, 0)])]
    pallas_call x1 -> x0, Pallas kernels: 1.75 us -> none  [spread(): pl.pallas_call(spread_kernel, out_shape=array(PEERS, rows, 128, dtype=jnp...]
    ppermute x0 -> x1, waiting for transfers between devices: none -> 1.22 us  [local(): theirs = lax.ppermute(mine, 'xh', [(0, 1), (1, 0)])]
    another operation x0 -> x1, local copies, waits for them, and re-layouts: none -> 0.77 us  [interleaved(): tiles = values.reshape(values.shape[0], 2, values.shape[2] // 128, 128)]
    broadcast_in_dim x0 -> x1, local copies, waits for them, and re-layouts: none -> 0.73 us  [local(): operand = jnp.broadcast_to(plane, (PEERS, 4 * PLANE, 128))]
    unnamed x8 -> x10, local copies, waits for them, and re-layouts: 0.02 us -> 0.67 us
    ppermute x1, waiting for transfers between devices: 0.99 us -> 0.37 us  [local(): swapped = lax.ppermute(gathered, 'core', [(0, 1), (1, 0)])]
  transfers between devices with their start and end apart: 2 -> 3, of which waited for: 2 -> 3; matrix products, arithmetic and copies ran while one was open for 0% -> 0% of each run, Pallas kernels for 1% -> 2%
where the time goes in v5:
time: 54.6 us; the launch traced here: 53.8 us
  blocking collectives  22 us (40%)
  starting transfers between devices  20.7 us (38%)
  Pallas kernels  4.26 us (8%)
  waiting for transfers between devices  3.78 us (7%)
  local copies, waits for them, and re-layouts  2.18 us (4%)
  between operations  0.75 us (1%)
    all_to_all x1, blocking collectives, local(): shares = lax.all_to_all(shares, ('xh', 'zz'), 0, 0, tiled=True)  22 us
    all_to_all x1, starting transfers between devices, local(): gathered = lax.all_to_all(operand, ('xh', 'chip'), 0, 0, tiled=True)  10.5 us
    ppermute x1, starting transfers between devices, local(): swapped = lax.ppermute(gathered, 'core', [(0, 1), (1, 0)])  5.61 us
    ppermute x1, starting transfers between devices, local(): theirs = lax.ppermute(mine, 'xh', [(0, 1), (1, 0)])  4.64 us
    pallas_call x4, Pallas kernels, call(): pl.pallas_call(kernel, out_shape=shapes, in_specs=specs, out_specs=jax.tr...  4.26 us
    all_to_all x1, waiting for transfers between devices, local(): gathered = lax.all_to_all(operand, ('xh', 'chip'), 0, 0, tiled=True)  2.19 us
    ppermute x1, waiting for transfers between devices, local(): theirs = lax.ppermute(mine, 'xh', [(0, 1), (1, 0)])  1.22 us
  transfers between devices with their start and end apart: 3, of which 3 were waited for; matrix products, arithmetic and copies ran while one was open for 0% of the time, Pallas kernels for 2%

profile of v5, /device:TPU:1, one launch (start us, length us, event | category | flops | bytes accessed | tf_op | source)
XLA Modules:
  0.0 53.8 jit_solution(13863756966627002116)
XLA Ops:
  0.0 0.0 copy-start.1
  0.0 0.8 %reshape_squeeze.6 = bf16[2,2,8,128]{3,2,1,0:T(8,128)(2,1)S(1)} reshape(bf16[1,2,2,1024]{3,2,1,0:T(2,128)(2,1)} %param.8) | data formatting | bytes 16384 | tf_op jit(solution)/shard_map/reshape;squeeze | solution.py:273
  0.8 0.7 %broadcast_in_dim.8 = bf16[32,32,128]{2,1,0:T(8,128)(2,1)} broadcast(bf16[32,128]{1,0:T(8,128)(2,1)S(1)} %bitcast.16), dimensions={1,2} | broadcast | bytes 270336 | tf_op jit(solution)/shard_map/broadcast_in_dim | solution.py:281
  1.5 10.5 %all-to-all-start = ((bf16[32,32,128]{2,1,0:T(8,128)(2,1)}), bf16[32,32,128]{2,1,0:T(8,128)(2,1)S(1)}, u32[]{:S(2)}, u32[]{:S(2)}) async-start(bf16[32,32,128]{2,1,0:T(8,128)(2,1)} %broadcast_in_dim.8), calls=%async_computation | async-start | bytes 524288 | tf_op jit(solution)/shard_map/all_to_all | solution.py:282
  12.7 0.0 copy-start.4
  12.7 0.6 %copy-done.4 = s32[1,1,3]{2,1,0:T(1,128)S(1)} copy-done((s32[1,1,3]{2,1,0:T(1,128)S(1)}, s32[1,1,3]{2,1,0:T(1,128)}, u32[]{:S(2)}) %copy-start.4) | copy-done | bytes 36
  13.3 0.1 pad_add_fusion.mine
  13.4 4.6 %collective-permute-start = (s32[1,5]{1,0:T(1,128)S(1)}, s32[1,5]{1,0:T(1,128)S(1)}, u32[]{:S(2)}, u32[]{:S(2)}) collective-permute-start(s32[1,5]{1,0:T(1,128)S(1)} %pad_add_fusion.mine), channel_id=1, source_target_pairs={{0,8},{8,0},{1,9},{9,1},{2,10},{10,2},{3,11},{11,3},{4,12},{12,4},... | collective-permute-start | bytes 68 | tf_op jit(solution)/shard_map/ppermute | solution.py:284
  18.0 0.0 copy-done.1
  18.1 0.0 copy-start
  18.1 0.0 copy-start.3
  18.1 0.2 apart.1.targets
  18.3 0.0 copy-start.2
  18.3 1.2 %collective-permute-done.theirs = s32[1,5]{1,0:T(1,128)S(1)} collective-permute-done((s32[1,5]{1,0:T(1,128)S(1)}, s32[1,5]{1,0:T(1,128)S(1)}, u32[]{:S(2)}, u32[]{:S(2)}) %collective-permute-start) | collective-permute-done | bytes 52 | tf_op jit(solution)/shard_map/ppermute | solution.py:284
  19.5 2.2 %all-to-all-done.own = bf16[32,32,128]{2,1,0:T(8,128)(2,1)S(1)} async-done(((bf16[32,32,128]{2,1,0:T(8,128)(2,1)}), bf16[32,32,128]{2,1,0:T(8,128)(2,1)S(1)}, u32[]{:S(2)}, u32[]{:S(2)}) %all-to-all-start) | async-done | bytes 262176 | tf_op jit(solution)/shard_map/all_to_all | solution.py:282
  21.7 5.6 %collective-permute-start.1 = (bf16[32,32,128]{2,1,0:T(8,128)(2,1)S(1)}, bf16[32,32,128]{2,1,0:T(8,128)(2,1)S(1)}, u32[]{:S(2)}, u32[]{:S(2)}) collective-permute-start(bf16[32,32,128]{2,1,0:T(8,128)(2,1)S(1)} %all-to-all-done.own), channel_id=1, source_target_pairs={{0,16},{16,0},{1,17},{17,1},{2,18},{18,2},{3,19},{19,3},{4,20},{20... | collective-permute-start | bytes 786440 | tf_op jit(solution)/shard_map/ppermute | solution.py:287
  27.3 0.8 %coulomb.1.kernel = f32[2,256,128]{2,1,0:T(8,128)S(1)} custom-call(s32[1,5]{1,0:T(1,128)S(1)} %pad_add_fusion.mine, s32[1,5]{1,0:T(1,128)S(1)} %collective-permute-done.theirs), custom_call_target="tpu_custom_call" | custom-call | tf_op jit(solution)/shard_map/coulomb/pallas_call | solution.py:233
  28.1 0.4 collective-permute-done.1.other
  28.5 0.0 copy-done
  28.5 0.0 copy-done.3
  28.5 0.0 copy-done.2
  28.5 2.4 %exchange.1 = bf16[16,72,128]{2,1,0:T(8,128)(2,1)S(1)} custom-call(s32[1,1]{1,0:T(1,128)} %bitcast.core, f32[2,256,128]{2,1,0:T(8,128)S(1)} %coulomb.1.kernel, f32[4,2,256,128]{3,2,1,0:T(8,128)S(1)} %apart.1.targets, bf16[32,32,128]{2,1,0:T(8,128)(2,1)S(1)} %all-to-all-done.own, bf16[32,32,128]{2,1,0:T(8,128)(2,1)S(1)} %collective-permute-done.1.other, ...), custom_call_target="tpu_custom_call" | custom-call | tf_op jit(solution)/shard_map/exchange/pallas_call | solution.py:233
  30.9 22.0 %all_to_all.10.shares = bf16[16,72,128]{2,1,0:T(8,128)(2,1)S(1)} all-to-all(bf16[16,72,128]{2,1,0:T(8,128)(2,1)S(1)} %exchange.1), channel_id=1, replica_groups=mesh['chip'=16,'core'=2,'xh'=2,'zz'=8] {'xh','zz'}, dimensions={0} | all-to-all | bytes 589824 | tf_op jit(solution)/shard_map/all_to_all | solution.py:290
  52.9 0.9 %projector.1 = f32[256,128]{1,0:T(8,128)} custom-call(bf16[16,72,128]{2,1,0:T(8,128)(2,1)S(1)} %all_to_all.10.shares), custom_call_target="tpu_custom_call" | custom-call | tf_op jit(solution)/shard_map/projector/pallas_call | solution.py:233
  (1 shorter events, 0.0 us)
Async XLA Ops:
  0.0 18.0 %copy-start.1 = (bf16[1,4,2,32768]{3,2,1,0:T(2,128)(2,1)S(1)}, bf16[1,4,2,32768]{3,2,1,0:T(2,128)(2,1)}, u32[]{:S(2)}) copy-start(bf16[1,4,2,32768]{3,2,1,0:T(2,128)(2,1)} %param.7) | copy-start | bytes 1572868
  1.5 20.2 %all-to-all-start = ((bf16[32,32,128]{2,1,0:T(8,128)(2,1)}), bf16[32,32,128]{2,1,0:T(8,128)(2,1)S(1)}, u32[]{:S(2)}, u32[]{:S(2)}) async-start(bf16[32,32,128]{2,1,0:T(8,128)(2,1)} %broadcast_in_dim.8), calls=%async_computation | async-start | bytes 524288 | tf_op jit(solution)/shard_map/all_to_all | solution.py:282
  12.7 0.7 %copy-start.4 = (s32[1,1,3]{2,1,0:T(1,128)S(1)}, s32[1,1,3]{2,1,0:T(1,128)}, u32[]{:S(2)}) copy-start(s32[1,1,3]{2,1,0:T(1,128)} %param.10) | copy-start | bytes 40
  13.4 6.1 %collective-permute-start = (s32[1,5]{1,0:T(1,128)S(1)}, s32[1,5]{1,0:T(1,128)S(1)}, u32[]{:S(2)}, u32[]{:S(2)}) collective-permute-start(s32[1,5]{1,0:T(1,128)S(1)} %pad_add_fusion.mine), channel_id=1, source_target_pairs={{0,8},{8,0},{1,9},{9,1},{2,10},{10,2},{3,11},{11,3},{4,12},{12,4},... | collective-permute-start | bytes 68 | tf_op jit(solution)/shard_map/ppermute | solution.py:284
  18.1 10.4 %copy-start = (bf16[512,512]{1,0:T(8,128)(2,1)S(1)}, bf16[512,512]{1,0:T(8,128)(2,1)}, u32[]{:S(2)}) copy-start(bf16[512,512]{1,0:T(8,128)(2,1)} %constant.16.clone.left) | copy-start | bytes 1572868
  18.1 10.4 %copy-start.3 = (bf16[256,256]{1,0:T(8,128)(2,1)S(1)}, bf16[256,256]{1,0:T(8,128)(2,1)}, u32[]{:S(2)}) copy-start(bf16[256,256]{1,0:T(8,128)(2,1)} %constant.17.clone.right) | copy-start | bytes 393220
  18.3 10.2 %copy-start.2 = (f32[2,256,128]{2,1,0:T(8,128)S(1)}, f32[2,256,128]{2,1,0:T(8,128)}, u32[]{:S(2)}) copy-start(f32[2,256,128]{2,1,0:T(8,128)} %constant.18.clone.twist) | copy-start | bytes 786436
  21.7 6.8 %collective-permute-start.1 = (bf16[32,32,128]{2,1,0:T(8,128)(2,1)S(1)}, bf16[32,32,128]{2,1,0:T(8,128)(2,1)S(1)}, u32[]{:S(2)}, u32[]{:S(2)}) collective-permute-start(bf16[32,32,128]{2,1,0:T(8,128)(2,1)S(1)} %all-to-all-done.own), channel_id=1, source_target_pairs={{0,16},{16,0},{1,17},{17,1},{2,18},{18,2},{3,19},{19,3},{4,20},{20... | collective-permute-start | bytes 786440 | tf_op jit(solution)/shard_map/ppermute | solution.py:287

commit v6 on v5

--- a/solution.py
+++ b/solution.py
@@ -6,6 +6,7 @@
 from jax.experimental.pallas import tpu as pltpu
 from jax.sharding import Mesh
 from jax.sharding import PartitionSpec as P
+
 
 GRID = 32
 BANDS = 4
@@ -229,7 +230,7 @@
 VMEM = pl.BlockSpec(memory_space=pltpu.VMEM)
 
 
-def call(kernel, name, shapes, specs, scratch, limit, *operands):
+def call(kernel, shapes, specs, scratch, limit, *operands):
     return pl.pallas_call(
         kernel,
         out_shape=shapes,
@@ -237,7 +238,6 @@
         out_specs=jax.tree.map(lambda _: VMEM, shapes),
         scratch_shapes=scratch,
         compiler_params=pltpu.CompilerParams(vmem_limit_bytes=limit << 20),
-        name=name,
     )(*operands)
 
 
@@ -246,13 +246,13 @@
 
 
 def prepare(mine, theirs):
-    return call(coulomb_kernel, "coulomb", array(2, ROWS, 128), [SMEM, SMEM], [], 2, mine, theirs)
+    return call(coulomb_kernel, array(2, ROWS, 128), [SMEM, SMEM], [], 2, mine, theirs)
 
 
 def apart(place, targets):
     scratch = [pltpu.VMEM((2 * ROWS, 128), jnp.float32)]
     shape = array(BANDS, 2, ROWS, 128)
-    return call(apart_kernel, "apart", shape, [SMEM, VMEM], scratch, 4, place, targets)
+    return call(apart_kernel, shape, [SMEM, VMEM], scratch, 4, place, targets)
 
 
 def exchange(*operands):
@@ -262,11 +262,11 @@
     ]
     shape = array(16, FIELD_ROWS + EXTRA, 128, dtype=jnp.bfloat16)
     specs = [SMEM] + [VMEM] * (len(operands) - 1)
-    return call(exchange_kernel, "exchange", shape, specs, scratch, 24, *operands)
+    return call(exchange_kernel, shape, specs, scratch, 24, *operands)
 
 
 def projector(shares):
-    return call(projector_kernel, "projector", array(256, 128), [VMEM], [], 4, shares)
+    return call(projector_kernel, array(256, 128), [VMEM], [], 4, shares)
 
 
 def interleaved(values):
@@ -283,7 +283,7 @@
     mine = jnp.concatenate([pair_map, shifts[0], group], 1)
     theirs = lax.ppermute(mine, "xh", [(0, 1), (1, 0)])
     parts = apart(group, interleaved(targets[0]))
-    gathered, parts, theirs = lax.optimization_barrier((gathered, parts, theirs))
+    gathered, parts = lax.optimization_barrier((gathered, parts))
     swapped = lax.ppermute(gathered, "core", [(0, 1), (1, 0)])
     kernel = prepare(mine, theirs)
     shares = exchange(core, kernel, parts, gathered, swapped, left, right, twist)

time: 54.6 us -> 60.7 us (1.11)
  the two profiles are of different devices: /device:TPU:1 before, /device:TPU:8 now
where the time goes in v6:
time: 60.7 us; the launch traced here: 60.3 us
  blocking collectives  22.6 us (37%)
  waiting for transfers between devices  15.7 us (26%)
  starting transfers between devices  15.3 us (25%)
  Pallas kernels  4.27 us (7%)
  local copies, waits for them, and re-layouts  1.54 us (3%)
  between operations  0.78 us (1%)
    all_to_all x1, blocking collectives, local(): shares = lax.all_to_all(shares, ('xh', 'zz'), 0, 0, tiled=True)  22.6 us
    all_to_all x1, waiting for transfers between devices, local(): gathered = lax.all_to_all(operand, ('xh', 'chip'), 0, 0, tiled=True)  12 us
    all_to_all x1, starting transfers between devices, local(): gathered = lax.all_to_all(operand, ('xh', 'chip'), 0, 0, tiled=True)  10.2 us
    pallas_call x4, Pallas kernels, call(): pl.pallas_call(kernel, out_shape=shapes, in_specs=specs, out_specs=jax.tr...  4.27 us
    ppermute x1, waiting for transfers between devices, local(): theirs = lax.ppermute(mine, 'xh', [(0, 1), (1, 0)])  3.72 us
    ppermute x1, starting transfers between devices, local(): theirs = lax.ppermute(mine, 'xh', [(0, 1), (1, 0)])  3.23 us
    ppermute x1, starting transfers between devices, local(): swapped = lax.ppermute(gathered, 'core', [(0, 1), (1, 0)])  1.91 us
  transfers between devices with their start and end apart: 3, of which 2 were waited for; matrix products, arithmetic and copies ran while one was open for 0% of the time, Pallas kernels for 2%

profile of v6, /device:TPU:8, one launch (start us, length us, event | category | flops | bytes accessed | tf_op | source)
XLA Modules:
  0.0 60.3 jit_solution(17288933431453013034)
XLA Ops:
  0.0 0.0 copy-start.1
  0.0 0.8 %reshape_squeeze.6 = bf16[2,2,8,128]{3,2,1,0:T(8,128)(2,1)S(1)} reshape(bf16[1,2,2,1024]{3,2,1,0:T(2,128)(2,1)} %param.8) | data formatting | bytes 16384 | tf_op jit(solution)/shard_map/reshape;squeeze | solution.py:273
  0.8 0.7 %broadcast_in_dim.8 = bf16[32,32,128]{2,1,0:T(8,128)(2,1)} broadcast(bf16[32,128]{1,0:T(8,128)(2,1)S(1)} %bitcast.16), dimensions={1,2} | broadcast | bytes 270336 | tf_op jit(solution)/shard_map/broadcast_in_dim | solution.py:281
  1.5 10.2 %all-to-all-start = ((bf16[32,32,128]{2,1,0:T(8,128)(2,1)}), bf16[32,32,128]{2,1,0:T(8,128)(2,1)S(1)}, u32[]{:S(2)}, u32[]{:S(2)}) async-start(bf16[32,32,128]{2,1,0:T(8,128)(2,1)} %broadcast_in_dim.8), calls=%async_computation | async-start | bytes 524288 | tf_op jit(solution)/shard_map/all_to_all | solution.py:282
  11.7 0.0 copy-done.1
  11.7 0.0 copy-start.4
  11.7 0.0 copy-start
  11.7 0.0 copy-start.3
  11.7 0.2 shard_map.74.targets
  11.9 0.0 copy-start.2
  11.9 12.0 %all-to-all-done.own = bf16[32,32,128]{2,1,0:T(8,128)(2,1)S(1)} async-done(((bf16[32,32,128]{2,1,0:T(8,128)(2,1)}), bf16[32,32,128]{2,1,0:T(8,128)(2,1)S(1)}, u32[]{:S(2)}, u32[]{:S(2)}) %all-to-all-start) | async-done | bytes 262176 | tf_op jit(solution)/shard_map/all_to_all | solution.py:282
  24.0 1.9 %collective-permute-start.1 = (bf16[32,32,128]{2,1,0:T(8,128)(2,1)S(1)}, bf16[32,32,128]{2,1,0:T(8,128)(2,1)S(1)}, u32[]{:S(2)}, u32[]{:S(2)}) collective-permute-start(bf16[32,32,128]{2,1,0:T(8,128)(2,1)S(1)} %all-to-all-done.own), channel_id=1, source_target_pairs={{0,16},{16,0},{1,17},{17,1},{2,18},{18,2},{3,19},{19,3},{4,20},{20... | collective-permute-start | bytes 786440 | tf_op jit(solution)/shard_map/ppermute | solution.py:287
  26.5 0.0 copy-done.4
  26.5 0.1 pad_add_fusion.mine
  26.6 3.2 %collective-permute-start = (s32[1,5]{1,0:T(1,128)S(1)}, s32[1,5]{1,0:T(1,128)S(1)}, u32[]{:S(2)}, u32[]{:S(2)}) collective-permute-start(s32[1,5]{1,0:T(1,128)S(1)} %pad_add_fusion.mine), channel_id=1, source_target_pairs={{0,8},{8,0},{1,9},{9,1},{2,10},{10,2},{3,11},{11,3},{4,12},{12,4},... | collective-permute-start | bytes 68 | tf_op jit(solution)/shard_map/ppermute | solution.py:284
  29.8 3.7 %collective-permute-done.theirs = s32[1,5]{1,0:T(1,128)S(1)} collective-permute-done((s32[1,5]{1,0:T(1,128)S(1)}, s32[1,5]{1,0:T(1,128)S(1)}, u32[]{:S(2)}, u32[]{:S(2)}) %collective-permute-start) | collective-permute-done | bytes 52 | tf_op jit(solution)/shard_map/ppermute | solution.py:284
  33.6 0.8 %shard_map.73.kernel = f32[2,256,128]{2,1,0:T(8,128)S(1)} custom-call(s32[1,5]{1,0:T(1,128)S(1)} %pad_add_fusion.mine, s32[1,5]{1,0:T(1,128)S(1)} %collective-permute-done.theirs), custom_call_target="tpu_custom_call" | custom-call | tf_op jit(solution)/shard_map/pallas_call | solution.py:234
  34.3 0.0 collective-permute-done.1.other
  34.3 0.0 copy-done
  34.4 0.0 copy-done.3
  34.4 0.0 copy-done.2
  34.4 2.5 %shard_map.75 = bf16[16,72,128]{2,1,0:T(8,128)(2,1)S(1)} custom-call(s32[1,1]{1,0:T(1,128)} %bitcast.core, f32[2,256,128]{2,1,0:T(8,128)S(1)} %shard_map.73.kernel, f32[4,2,256,128]{3,2,1,0:T(8,128)S(1)} %shard_map.74.targets, bf16[32,32,128]{2,1,0:T(8,128)(2,1)S(1)} %all-to-all-done.own, bf16[32,32,128]{2,1,0:T(8,128)(2,1)S(1)} %collective-permute-done.1.other, ...), custom_call_target="tpu_custom_call" | custom-call | tf_op jit(solution)/shard_map/pallas_call | solution.py:234
  36.8 22.6 %all_to_all.10.shares = bf16[16,72,128]{2,1,0:T(8,128)(2,1)S(1)} all-to-all(bf16[16,72,128]{2,1,0:T(8,128)(2,1)S(1)} %shard_map.75), channel_id=1, replica_groups=mesh['chip'=16,'core'=2,'xh'=2,'zz'=8] {'xh','zz'}, dimensions={0} | all-to-all | bytes 589824 | tf_op jit(solution)/shard_map/all_to_all | solution.py:290
  59.5 0.9 %shard_map.76 = f32[256,128]{1,0:T(8,128)} custom-call(bf16[16,72,128]{2,1,0:T(8,128)(2,1)S(1)} %all_to_all.10.shares), custom_call_target="tpu_custom_call" | custom-call | tf_op jit(solution)/shard_map/pallas_call | solution.py:234
  (1 shorter events, 0.0 us)
Async XLA Ops:
  0.0 11.7 %copy-start.1 = (bf16[1,4,2,32768]{3,2,1,0:T(2,128)(2,1)S(1)}, bf16[1,4,2,32768]{3,2,1,0:T(2,128)(2,1)}, u32[]{:S(2)}) copy-start(bf16[1,4,2,32768]{3,2,1,0:T(2,128)(2,1)} %param.7) | copy-start | bytes 1572868
  1.5 22.4 %all-to-all-start = ((bf16[32,32,128]{2,1,0:T(8,128)(2,1)}), bf16[32,32,128]{2,1,0:T(8,128)(2,1)S(1)}, u32[]{:S(2)}, u32[]{:S(2)}) async-start(bf16[32,32,128]{2,1,0:T(8,128)(2,1)} %broadcast_in_dim.8), calls=%async_computation | async-start | bytes 524288 | tf_op jit(solution)/shard_map/all_to_all | solution.py:282
  11.7 14.8 %copy-start.4 = (s32[1,1,3]{2,1,0:T(1,128)S(1)}, s32[1,1,3]{2,1,0:T(1,128)}, u32[]{:S(2)}) copy-start(s32[1,1,3]{2,1,0:T(1,128)} %param.10) | copy-start | bytes 40
  11.7 22.6 %copy-start = (bf16[512,512]{1,0:T(8,128)(2,1)S(1)}, bf16[512,512]{1,0:T(8,128)(2,1)}, u32[]{:S(2)}) copy-start(bf16[512,512]{1,0:T(8,128)(2,1)} %constant.16.clone.left) | copy-start | bytes 1572868
  11.7 22.6 %copy-start.3 = (bf16[256,256]{1,0:T(8,128)(2,1)S(1)}, bf16[256,256]{1,0:T(8,128)(2,1)}, u32[]{:S(2)}) copy-start(bf16[256,256]{1,0:T(8,128)(2,1)} %constant.17.clone.right) | copy-start | bytes 393220
  11.9 22.4 %copy-start.2 = (f32[2,256,128]{2,1,0:T(8,128)S(1)}, f32[2,256,128]{2,1,0:T(8,128)}, u32[]{:S(2)}) copy-start(f32[2,256,128]{2,1,0:T(8,128)} %constant.18.clone.twist) | copy-start | bytes 786436
  24.0 10.4 %collective-permute-start.1 = (bf16[32,32,128]{2,1,0:T(8,128)(2,1)S(1)}, bf16[32,32,128]{2,1,0:T(8,128)(2,1)S(1)}, u32[]{:S(2)}, u32[]{:S(2)}) collective-permute-start(bf16[32,32,128]{2,1,0:T(8,128)(2,1)S(1)} %all-to-all-done.own), channel_id=1, source_target_pairs={{0,16},{16,0},{1,17},{17,1},{2,18},{18,2},{3,19},{19,3},{4,20},{20... | collective-permute-start | bytes 786440 | tf_op jit(solution)/shard_map/ppermute | solution.py:287
  26.6 7.0 %collective-permute-start = (s32[1,5]{1,0:T(1,128)S(1)}, s32[1,5]{1,0:T(1,128)S(1)}, u32[]{:S(2)}, u32[]{:S(2)}) collective-permute-start(s32[1,5]{1,0:T(1,128)S(1)} %pad_add_fusion.mine), channel_id=1, source_target_pairs={{0,8},{8,0},{1,9},{9,1},{2,10},{10,2},{3,11},{11,3},{4,12},{12,4},... | collective-permute-start | bytes 68 | tf_op jit(solution)/shard_map/ppermute | solution.py:284

commit v7 on v5

--- a/solution.py
+++ b/solution.py
@@ -19,6 +19,8 @@
 FIELD_ROWS = 32 * OWN
 EXTRA = 8
 PEERS = 32
+PLANE_FIRST = 20
+SUM_FIRST = 12
 PAIRS = [(0, 0, 0), (1, 1, 0), (0, 1, 0), (0, 1, 1), (2, 0, 0), (2, 0, 1), (3, 1, 0), (3, 1, 1)]
 
 
@@ -57,6 +59,10 @@
     return KPOINT_SCALING / (squared + SCREENING_CUTOFF)
 
 
+def order(count, first):
+    return [[at ^ first for at in range(count)]]
+
+
 def product(a, b):
     return jnp.dot(a, b, preferred_element_type=jnp.float32)
 
@@ -83,8 +89,10 @@
     for source, parity in ((own, core[0, 0]), (other, 1 - core[0, 0])):
         for q in range(2):
             for j in range(OCC):
-                planes = source[16 * q : 16 * q + 16, 16 * j : 16 * j + 16].astype(jnp.float32)
-                rows[q, j, :, pl.ds(parity, 1)] = planes[:, None]
+                for m in range(0, 16, 4):
+                    at = (16 * q + m) ^ PLANE_FIRST
+                    planes = source[at : at + 4, 16 * j : 16 * j + 16].astype(jnp.float32)
+                    rows[q, j, m : m + 4, pl.ds(parity, 1)] = planes[:, None]
     for q in range(2):
         for j in range(OCC):
             for part in range(2):
@@ -150,8 +158,12 @@
     sums = {}
     for band in range(OWN):
         re, im = field(values[OCC * band : OCC * band + OCC])
-        out[:, 32 * band : 32 * band + 16] = re.astype(jnp.bfloat16).reshape(16, 16, 128)
-        out[:, 32 * band + 16 : 32 * band + 32] = im.astype(jnp.bfloat16).reshape(16, 16, 128)
+        for part, value in enumerate((re, im)):
+            value = value.astype(jnp.bfloat16).reshape(16, 16, 128)
+            first = 32 * band + 16 * part
+            for to in range(0, 16, 4):
+                at = to ^ SUM_FIRST
+                out[at : at + 4, first : first + 16] = value[to : to + 4]
         for slot, place, cross in PAIRS:
             if place == band:
                 if cross:
@@ -172,9 +184,9 @@
 def projector_kernel(shares, out):
     totals = []
     for group in range(2):
-        total = shares[8 * group].astype(jnp.float32)
+        total = shares[(8 * group) ^ SUM_FIRST].astype(jnp.float32)
         for source in range(8 * group + 1, 8 * group + 8):
-            total += shares[source].astype(jnp.float32)
+            total += shares[source ^ SUM_FIRST].astype(jnp.float32)
         totals.append(total)
     value = {}
     for group in range(2):
@@ -279,7 +291,9 @@
     core, group = (lax.axis_index(axis).reshape(1, 1) for axis in ("core", "xh"))
     plane = interleaved(partners[0]).reshape(1, 4 * PLANE, 128)
     operand = jnp.broadcast_to(plane, (PEERS, 4 * PLANE, 128))
-    gathered = lax.all_to_all(operand, ("xh", "chip"), 0, 0, tiled=True)
+    gathered = lax.all_to_all(
+        operand, ("xh", "chip"), 0, 0, axis_index_groups=order(PEERS, PLANE_FIRST), tiled=True
+    )
     mine = jnp.concatenate([pair_map, shifts[0], group], 1)
     theirs = lax.ppermute(mine, "xh", [(0, 1), (1, 0)])
     parts = apart(group, interleaved(targets[0]))
@@ -287,7 +301,9 @@
     swapped = lax.ppermute(gathered, "core", [(0, 1), (1, 0)])
     kernel = prepare(mine, theirs)
     shares = exchange(core, kernel, parts, gathered, swapped, left, right, twist)
-    shares = lax.all_to_all(shares, ("xh", "zz"), 0, 0, tiled=True)
+    shares = lax.all_to_all(
+        shares, ("xh", "zz"), 0, 0, axis_index_groups=order(16, SUM_FIRST), tiled=True
+    )
     rows = projector(shares).reshape(2 * BANDS, 16, 2, 128)
     return jnp.swapaxes(rows, 1, 2).reshape(1, 2 * BANDS, 2, 2048)
 

time: 54.6 us -> 52.7 us (0.965)
  blocking collectives: 22 us -> 19.5 us
  starting transfers between devices: 20.7 us -> 21.4 us
    ppermute x1, waiting for transfers between devices: 1.22 us -> 3.82 us  [local(): theirs = lax.ppermute(mine, 'xh', [(0, 1), (1, 0)])]
    ppermute x1, starting transfers between devices: 4.64 us -> 2.07 us  [local(): theirs = lax.ppermute(mine, 'xh', [(0, 1), (1, 0)])]
    all_to_all x1, blocking collectives: 22 us -> 19.5 us  [local(): lax.all_to_all(shares, ('xh', 'zz'), 0, 0, axis_index_groups=order(16, SU...]
    all_to_all x1, waiting for transfers between devices: 2.19 us -> 0.01 us  [local(): lax.all_to_all(operand, ('xh', 'chip'), 0, 0, axis_index_groups=order(PEE...]
    all_to_all x1, starting transfers between devices: 10.5 us -> 12.5 us  [local(): lax.all_to_all(operand, ('xh', 'chip'), 0, 0, axis_index_groups=order(PEE...]
    ppermute x1, starting transfers between devices: 5.61 us -> 6.87 us  [local(): swapped = lax.ppermute(gathered, 'core', [(0, 1), (1, 0)])]
  transfers between devices with their start and end apart: 3 -> 3, of which waited for: 3 -> 2; matrix products, arithmetic and copies ran while one was open for 0% -> 0% of each run, Pallas kernels for 2% -> 2%
where the time goes in v7:
time: 52.7 us; the launch traced here: 52.4 us
  starting transfers between devices  21.4 us (41%)
  blocking collectives  19.5 us (37%)
  Pallas kernels  4.27 us (8%)
  waiting for transfers between devices  4.2 us (8%)
  local copies, waits for them, and re-layouts  2.18 us (4%)
  between operations  0.75 us (1%)
    all_to_all x1, blocking collectives, local(): lax.all_to_all(shares, ('xh', 'zz'), 0, 0, axis_index_groups=order(16, SU...  19.5 us
    all_to_all x1, starting transfers between devices, local(): lax.all_to_all(operand, ('xh', 'chip'), 0, 0, axis_index_groups=order(PEE...  12.5 us
    ppermute x1, starting transfers between devices, local(): swapped = lax.ppermute(gathered, 'core', [(0, 1), (1, 0)])  6.87 us
    pallas_call x4, Pallas kernels, call(): pl.pallas_call(kernel, out_shape=shapes, in_specs=specs, out_specs=jax.tr...  4.27 us
    ppermute x1, waiting for transfers between devices, local(): theirs = lax.ppermute(mine, 'xh', [(0, 1), (1, 0)])  3.82 us
    ppermute x1, starting transfers between devices, local(): theirs = lax.ppermute(mine, 'xh', [(0, 1), (1, 0)])  2.07 us
  transfers between devices with their start and end apart: 3, of which 2 were waited for; matrix products, arithmetic and copies ran while one was open for 0% of the time, Pallas kernels for 2%

profile of v7, /device:TPU:1, one launch (start us, length us, event | category | flops | bytes accessed | tf_op | source)
XLA Modules:
  0.0 52.4 jit_solution(16284145397135212440)
XLA Ops:
  0.0 0.0 copy-start.1
  0.0 0.8 %reshape_squeeze.6 = bf16[2,2,8,128]{3,2,1,0:T(8,128)(2,1)S(1)} reshape(bf16[1,2,2,1024]{3,2,1,0:T(2,128)(2,1)} %param.8) | data formatting | bytes 16384 | tf_op jit(solution)/shard_map/reshape;squeeze | solution.py:285
  0.8 0.7 %broadcast_in_dim.8 = bf16[32,32,128]{2,1,0:T(8,128)(2,1)} broadcast(bf16[32,128]{1,0:T(8,128)(2,1)S(1)} %bitcast.16), dimensions={1,2} | broadcast | bytes 270336 | tf_op jit(solution)/shard_map/broadcast_in_dim | solution.py:293
  1.5 12.5 %all-to-all-start = ((bf16[32,32,128]{2,1,0:T(8,128)(2,1)}), bf16[32,32,128]{2,1,0:T(8,128)(2,1)S(1)}, u32[]{:S(2)}, u32[]{:S(2)}) async-start(bf16[32,32,128]{2,1,0:T(8,128)(2,1)} %broadcast_in_dim.8), calls=%async_computation | async-start | bytes 524288 | tf_op jit(solution)/shard_map/all_to_all | solution.py:294
  14.6 0.0 copy-start.4
  14.7 0.6 %copy-done.4 = s32[1,1,3]{2,1,0:T(1,128)S(1)} copy-done((s32[1,1,3]{2,1,0:T(1,128)S(1)}, s32[1,1,3]{2,1,0:T(1,128)}, u32[]{:S(2)}) %copy-start.4) | copy-done | bytes 36
  15.3 0.1 pad_add_fusion.mine
  15.4 2.1 %collective-permute-start = (s32[1,5]{1,0:T(1,128)S(1)}, s32[1,5]{1,0:T(1,128)S(1)}, u32[]{:S(2)}, u32[]{:S(2)}) collective-permute-start(s32[1,5]{1,0:T(1,128)S(1)} %pad_add_fusion.mine), channel_id=1, source_target_pairs={{0,8},{8,0},{1,9},{9,1},{2,10},{10,2},{3,11},{11,3},{4,12},{12,4},... | collective-permute-start | bytes 68 | tf_op jit(solution)/shard_map/ppermute | solution.py:298
  17.5 0.0 copy-done.1
  17.5 0.0 copy-start
  17.5 0.0 copy-start.3
  17.5 0.2 apart.1.targets
  17.7 0.0 copy-start.2
  17.7 3.8 %collective-permute-done.theirs = s32[1,5]{1,0:T(1,128)S(1)} collective-permute-done((s32[1,5]{1,0:T(1,128)S(1)}, s32[1,5]{1,0:T(1,128)S(1)}, u32[]{:S(2)}, u32[]{:S(2)}) %collective-permute-start) | collective-permute-done | bytes 52 | tf_op jit(solution)/shard_map/ppermute | solution.py:298
  21.5 0.0 all-to-all-done.own
  21.5 6.9 %collective-permute-start.1 = (bf16[32,32,128]{2,1,0:T(8,128)(2,1)S(1)}, bf16[32,32,128]{2,1,0:T(8,128)(2,1)S(1)}, u32[]{:S(2)}, u32[]{:S(2)}) collective-permute-start(bf16[32,32,128]{2,1,0:T(8,128)(2,1)S(1)} %all-to-all-done.own), channel_id=1, source_target_pairs={{0,16},{16,0},{1,17},{17,1},{2,18},{18,2},{3,19},{19,3},{4,20},{20... | collective-permute-start | bytes 786440 | tf_op jit(solution)/shard_map/ppermute | solution.py:301
  28.4 0.8 %coulomb.1.kernel = f32[2,256,128]{2,1,0:T(8,128)S(1)} custom-call(s32[1,5]{1,0:T(1,128)S(1)} %pad_add_fusion.mine, s32[1,5]{1,0:T(1,128)S(1)} %collective-permute-done.theirs), custom_call_target="tpu_custom_call" | custom-call | tf_op jit(solution)/shard_map/coulomb/pallas_call | solution.py:245
  29.2 0.4 collective-permute-done.1.other
  29.5 0.0 copy-done
  29.5 0.0 copy-done.3
  29.5 0.0 copy-done.2
  29.5 2.5 %exchange.1 = bf16[16,72,128]{2,1,0:T(8,128)(2,1)S(1)} custom-call(s32[1,1]{1,0:T(1,128)} %bitcast.core, f32[2,256,128]{2,1,0:T(8,128)S(1)} %coulomb.1.kernel, f32[4,2,256,128]{3,2,1,0:T(8,128)S(1)} %apart.1.targets, bf16[32,32,128]{2,1,0:T(8,128)(2,1)S(1)} %all-to-all-done.own, bf16[32,32,128]{2,1,0:T(8,128)(2,1)S(1)} %collective-permute-done.1.other, ...), custom_call_target="tpu_custom_call" | custom-call | tf_op jit(solution)/shard_map/exchange/pallas_call | solution.py:245
  32.0 19.5 %all_to_all.10.shares = bf16[16,72,128]{2,1,0:T(8,128)(2,1)S(1)} all-to-all(bf16[16,72,128]{2,1,0:T(8,128)(2,1)S(1)} %exchange.1), channel_id=1, replica_groups={{12,13,14,15,8,9,10,11,4,5,6,7,0,1,2,3},{28,29,30,31,24,25,26,27,20,21,..., dimensions={0} | all-to-all | bytes 589824 | tf_op jit(solution)/shard_map/all_to_all | solution.py:304
  51.5 0.9 %projector.1 = f32[256,128]{1,0:T(8,128)} custom-call(bf16[16,72,128]{2,1,0:T(8,128)(2,1)S(1)} %all_to_all.10.shares), custom_call_target="tpu_custom_call" | custom-call | tf_op jit(solution)/shard_map/projector/pallas_call | solution.py:245
  (1 shorter events, 0.0 us)
Async XLA Ops:
  0.0 17.5 %copy-start.1 = (bf16[1,4,2,32768]{3,2,1,0:T(2,128)(2,1)S(1)}, bf16[1,4,2,32768]{3,2,1,0:T(2,128)(2,1)}, u32[]{:S(2)}) copy-start(bf16[1,4,2,32768]{3,2,1,0:T(2,128)(2,1)} %param.7) | copy-start | bytes 1572868
  1.5 20.0 %all-to-all-start = ((bf16[32,32,128]{2,1,0:T(8,128)(2,1)}), bf16[32,32,128]{2,1,0:T(8,128)(2,1)S(1)}, u32[]{:S(2)}, u32[]{:S(2)}) async-start(bf16[32,32,128]{2,1,0:T(8,128)(2,1)} %broadcast_in_dim.8), calls=%async_computation | async-start | bytes 524288 | tf_op jit(solution)/shard_map/all_to_all | solution.py:294
  14.6 0.7 %copy-start.4 = (s32[1,1,3]{2,1,0:T(1,128)S(1)}, s32[1,1,3]{2,1,0:T(1,128)}, u32[]{:S(2)}) copy-start(s32[1,1,3]{2,1,0:T(1,128)} %param.10) | copy-start | bytes 40
  15.4 6.1 %collective-permute-start = (s32[1,5]{1,0:T(1,128)S(1)}, s32[1,5]{1,0:T(1,128)S(1)}, u32[]{:S(2)}, u32[]{:S(2)}) collective-permute-start(s32[1,5]{1,0:T(1,128)S(1)} %pad_add_fusion.mine), channel_id=1, source_target_pairs={{0,8},{8,0},{1,9},{9,1},{2,10},{10,2},{3,11},{11,3},{4,12},{12,4},... | collective-permute-start | bytes 68 | tf_op jit(solution)/shard_map/ppermute | solution.py:298
  17.5 12.1 %copy-start = (bf16[512,512]{1,0:T(8,128)(2,1)S(1)}, bf16[512,512]{1,0:T(8,128)(2,1)}, u32[]{:S(2)}) copy-start(bf16[512,512]{1,0:T(8,128)(2,1)} %constant.16.clone.left) | copy-start | bytes 1572868
  17.5 12.1 %copy-start.3 = (bf16[256,256]{1,0:T(8,128)(2,1)S(1)}, bf16[256,256]{1,0:T(8,128)(2,1)}, u32[]{:S(2)}) copy-start(bf16[256,256]{1,0:T(8,128)(2,1)} %constant.17.clone.right) | copy-start | bytes 393220
  17.7 11.9 %copy-start.2 = (f32[2,256,128]{2,1,0:T(8,128)S(1)}, f32[2,256,128]{2,1,0:T(8,128)}, u32[]{:S(2)}) copy-start(f32[2,256,128]{2,1,0:T(8,128)} %constant.18.clone.twist) | copy-start | bytes 786436
  21.5 8.0 %collective-permute-start.1 = (bf16[32,32,128]{2,1,0:T(8,128)(2,1)S(1)}, bf16[32,32,128]{2,1,0:T(8,128)(2,1)S(1)}, u32[]{:S(2)}, u32[]{:S(2)}) collective-permute-start(bf16[32,32,128]{2,1,0:T(8,128)(2,1)S(1)} %all-to-all-done.own), channel_id=1, source_target_pairs={{0,16},{16,0},{1,17},{17,1},{2,18},{18,2},{3,19},{19,3},{4,20},{20... | collective-permute-start | bytes 786440 | tf_op jit(solution)/shard_map/ppermute | solution.py:301

commit v8 on v7

--- a/solution.py
+++ b/solution.py
@@ -6,6 +6,7 @@
 from jax.experimental.pallas import tpu as pltpu
 from jax.sharding import Mesh
 from jax.sharding import PartitionSpec as P
+
 
 GRID = 32
 BANDS = 4
@@ -241,7 +242,7 @@
 VMEM = pl.BlockSpec(memory_space=pltpu.VMEM)
 
 
-def call(kernel, name, shapes, specs, scratch, limit, *operands):
+def call(kernel, shapes, specs, scratch, limit, *operands):
     return pl.pallas_call(
         kernel,
         out_shape=shapes,
@@ -249,7 +250,6 @@
         out_specs=jax.tree.map(lambda _: VMEM, shapes),
         scratch_shapes=scratch,
         compiler_params=pltpu.CompilerParams(vmem_limit_bytes=limit << 20),
-        name=name,
     )(*operands)
 
 
@@ -258,13 +258,13 @@
 
 
 def prepare(mine, theirs):
-    return call(coulomb_kernel, "coulomb", array(2, ROWS, 128), [SMEM, SMEM], [], 2, mine, theirs)
+    return call(coulomb_kernel, array(2, ROWS, 128), [SMEM, SMEM], [], 2, mine, theirs)
 
 
 def apart(place, targets):
     scratch = [pltpu.VMEM((2 * ROWS, 128), jnp.float32)]
     shape = array(BANDS, 2, ROWS, 128)
-    return call(apart_kernel, "apart", shape, [SMEM, VMEM], scratch, 4, place, targets)
+    return call(apart_kernel, shape, [SMEM, VMEM], scratch, 4, place, targets)
 
 
 def exchange(*operands):
@@ -274,11 +274,11 @@
     ]
     shape = array(16, FIELD_ROWS + EXTRA, 128, dtype=jnp.bfloat16)
     specs = [SMEM] + [VMEM] * (len(operands) - 1)
-    return call(exchange_kernel, "exchange", shape, specs, scratch, 24, *operands)
+    return call(exchange_kernel, shape, specs, scratch, 24, *operands)
 
 
 def projector(shares):
-    return call(projector_kernel, "projector", array(256, 128), [VMEM], [], 4, shares)
+    return call(projector_kernel, array(256, 128), [VMEM], [], 4, shares)
 
 
 def interleaved(values):
@@ -297,7 +297,7 @@
     mine = jnp.concatenate([pair_map, shifts[0], group], 1)
     theirs = lax.ppermute(mine, "xh", [(0, 1), (1, 0)])
     parts = apart(group, interleaved(targets[0]))
-    gathered, parts, theirs = lax.optimization_barrier((gathered, parts, theirs))
+    gathered, parts = lax.optimization_barrier((gathered, parts))
     swapped = lax.ppermute(gathered, "core", [(0, 1), (1, 0)])
     kernel = prepare(mine, theirs)
     shares = exchange(core, kernel, parts, gathered, swapped, left, right, twist)

time: 52.7 us -> 56.6 us (1.074)
  starting transfers between devices: 21.4 us -> 24.1 us
  blocking collectives: 19.5 us -> 20.8 us
  local copies, waits for them, and re-layouts: 2.18 us -> 1.54 us
    all_to_all x1, waiting for transfers between devices: 0.01 us -> 3.61 us  [local(): lax.all_to_all(operand, ('xh', 'chip'), 0, 0, axis_index_groups=order(PEE...]
    ppermute x1, waiting for transfers between devices: 3.82 us -> 1.05 us  [local(): theirs = lax.ppermute(mine, 'xh', [(0, 1), (1, 0)])]
    ppermute x1, starting transfers between devices: 2.07 us -> 4.74 us  [local(): theirs = lax.ppermute(mine, 'xh', [(0, 1), (1, 0)])]
    all_to_all x1, blocking collectives: 19.5 us -> 20.8 us  [local(): lax.all_to_all(shares, ('xh', 'zz'), 0, 0, axis_index_groups=order(16, SU...]
    unnamed x10, local copies, waits for them, and re-layouts: 0.67 us -> 0.03 us
where the time goes in v8:
time: 56.6 us; the launch traced here: 56.3 us
  starting transfers between devices  24.1 us (43%)
  blocking collectives  20.8 us (37%)
  waiting for transfers between devices  4.67 us (8%)
  Pallas kernels  4.27 us (8%)
  local copies, waits for them, and re-layouts  1.54 us (3%)
  between operations  0.78 us (1%)
    all_to_all x1, blocking collectives, local(): lax.all_to_all(shares, ('xh', 'zz'), 0, 0, axis_index_groups=order(16, SU...  20.8 us
    all_to_all x1, starting transfers between devices, local(): lax.all_to_all(operand, ('xh', 'chip'), 0, 0, axis_index_groups=order(PEE...  12.5 us
    ppermute x1, starting transfers between devices, local(): swapped = lax.ppermute(gathered, 'core', [(0, 1), (1, 0)])  6.91 us
    ppermute x1, starting transfers between devices, local(): theirs = lax.ppermute(mine, 'xh', [(0, 1), (1, 0)])  4.74 us
    pallas_call x4, Pallas kernels, call(): pl.pallas_call(kernel, out_shape=shapes, in_specs=specs, out_specs=jax.tr...  4.27 us
    all_to_all x1, waiting for transfers between devices, local(): lax.all_to_all(operand, ('xh', 'chip'), 0, 0, axis_index_groups=order(PEE...  3.61 us
  transfers between devices with their start and end apart: 3, of which 2 were waited for; matrix products, arithmetic and copies ran while one was open for 0% of the time, Pallas kernels for 2%

profile of v8, /device:TPU:1, one launch (start us, length us, event | category | flops | bytes accessed | tf_op | source)
XLA Modules:
  0.0 56.3 jit_solution(17105249033794498605)
XLA Ops:
  0.0 0.0 copy-start.1
  0.0 0.8 %reshape_squeeze.6 = bf16[2,2,8,128]{3,2,1,0:T(8,128)(2,1)S(1)} reshape(bf16[1,2,2,1024]{3,2,1,0:T(2,128)(2,1)} %param.8) | data formatting | bytes 16384 | tf_op jit(solution)/shard_map/reshape;squeeze | solution.py:285
  0.8 0.7 %broadcast_in_dim.8 = bf16[32,32,128]{2,1,0:T(8,128)(2,1)} broadcast(bf16[32,128]{1,0:T(8,128)(2,1)S(1)} %bitcast.16), dimensions={1,2} | broadcast | bytes 270336 | tf_op jit(solution)/shard_map/broadcast_in_dim | solution.py:293
  1.5 12.5 %all-to-all-start = ((bf16[32,32,128]{2,1,0:T(8,128)(2,1)}), bf16[32,32,128]{2,1,0:T(8,128)(2,1)S(1)}, u32[]{:S(2)}, u32[]{:S(2)}) async-start(bf16[32,32,128]{2,1,0:T(8,128)(2,1)} %broadcast_in_dim.8), calls=%async_computation | async-start | bytes 524288 | tf_op jit(solution)/shard_map/all_to_all | solution.py:294
  14.0 0.0 copy-done.1
  14.0 0.0 copy-start.4
  14.0 0.0 copy-start
  14.0 0.0 copy-start.3
  14.0 0.2 shard_map.74.targets
  14.2 0.0 copy-start.2
  14.2 3.6 %all-to-all-done.own = bf16[32,32,128]{2,1,0:T(8,128)(2,1)S(1)} async-done(((bf16[32,32,128]{2,1,0:T(8,128)(2,1)}), bf16[32,32,128]{2,1,0:T(8,128)(2,1)S(1)}, u32[]{:S(2)}, u32[]{:S(2)}) %all-to-all-start) | async-done | bytes 262176 | tf_op jit(solution)/shard_map/all_to_all | solution.py:294
  17.9 6.9 %collective-permute-start.1 = (bf16[32,32,128]{2,1,0:T(8,128)(2,1)S(1)}, bf16[32,32,128]{2,1,0:T(8,128)(2,1)S(1)}, u32[]{:S(2)}, u32[]{:S(2)}) collective-permute-start(bf16[32,32,128]{2,1,0:T(8,128)(2,1)S(1)} %all-to-all-done.own), channel_id=1, source_target_pairs={{0,16},{16,0},{1,17},{17,1},{2,18},{18,2},{3,19},{19,3},{4,20},{20... | collective-permute-start | bytes 786440 | tf_op jit(solution)/shard_map/ppermute | solution.py:301
  25.4 0.0 copy-done.4
  25.4 0.1 pad_add_fusion.mine
  25.5 4.7 %collective-permute-start = (s32[1,5]{1,0:T(1,128)S(1)}, s32[1,5]{1,0:T(1,128)S(1)}, u32[]{:S(2)}, u32[]{:S(2)}) collective-permute-start(s32[1,5]{1,0:T(1,128)S(1)} %pad_add_fusion.mine), channel_id=1, source_target_pairs={{0,8},{8,0},{1,9},{9,1},{2,10},{10,2},{3,11},{11,3},{4,12},{12,4},... | collective-permute-start | bytes 68 | tf_op jit(solution)/shard_map/ppermute | solution.py:298
  30.3 1.1 %collective-permute-done.theirs = s32[1,5]{1,0:T(1,128)S(1)} collective-permute-done((s32[1,5]{1,0:T(1,128)S(1)}, s32[1,5]{1,0:T(1,128)S(1)}, u32[]{:S(2)}, u32[]{:S(2)}) %collective-permute-start) | collective-permute-done | bytes 52 | tf_op jit(solution)/shard_map/ppermute | solution.py:298
  31.3 0.8 %shard_map.73.kernel = f32[2,256,128]{2,1,0:T(8,128)S(1)} custom-call(s32[1,5]{1,0:T(1,128)S(1)} %pad_add_fusion.mine, s32[1,5]{1,0:T(1,128)S(1)} %collective-permute-done.theirs), custom_call_target="tpu_custom_call" | custom-call | tf_op jit(solution)/shard_map/pallas_call | solution.py:246
  32.1 0.0 collective-permute-done.1.other
  32.1 0.0 copy-done
  32.1 0.0 copy-done.3
  32.1 0.0 copy-done.2
  32.1 2.5 %shard_map.75 = bf16[16,72,128]{2,1,0:T(8,128)(2,1)S(1)} custom-call(s32[1,1]{1,0:T(1,128)} %bitcast.core, f32[2,256,128]{2,1,0:T(8,128)S(1)} %shard_map.73.kernel, f32[4,2,256,128]{3,2,1,0:T(8,128)S(1)} %shard_map.74.targets, bf16[32,32,128]{2,1,0:T(8,128)(2,1)S(1)} %all-to-all-done.own, bf16[32,32,128]{2,1,0:T(8,128)(2,1)S(1)} %collective-permute-done.1.other, ...), custom_call_target="tpu_custom_call" | custom-call | tf_op jit(solution)/shard_map/pallas_call | solution.py:246
  34.6 20.8 %all_to_all.10.shares = bf16[16,72,128]{2,1,0:T(8,128)(2,1)S(1)} all-to-all(bf16[16,72,128]{2,1,0:T(8,128)(2,1)S(1)} %shard_map.75), channel_id=1, replica_groups={{12,13,14,15,8,9,10,11,4,5,6,7,0,1,2,3},{28,29,30,31,24,25,26,27,20,21,..., dimensions={0} | all-to-all | bytes 589824 | tf_op jit(solution)/shard_map/all_to_all | solution.py:304
  55.4 0.9 %shard_map.76 = f32[256,128]{1,0:T(8,128)} custom-call(bf16[16,72,128]{2,1,0:T(8,128)(2,1)S(1)} %all_to_all.10.shares), custom_call_target="tpu_custom_call" | custom-call | tf_op jit(solution)/shard_map/pallas_call | solution.py:246
  (1 shorter events, 0.0 us)
Async XLA Ops:
  0.0 14.0 %copy-start.1 = (bf16[1,4,2,32768]{3,2,1,0:T(2,128)(2,1)S(1)}, bf16[1,4,2,32768]{3,2,1,0:T(2,128)(2,1)}, u32[]{:S(2)}) copy-start(bf16[1,4,2,32768]{3,2,1,0:T(2,128)(2,1)} %param.7) | copy-start | bytes 1572868
  1.5 16.3 %all-to-all-start = ((bf16[32,32,128]{2,1,0:T(8,128)(2,1)}), bf16[32,32,128]{2,1,0:T(8,128)(2,1)S(1)}, u32[]{:S(2)}, u32[]{:S(2)}) async-start(bf16[32,32,128]{2,1,0:T(8,128)(2,1)} %broadcast_in_dim.8), calls=%async_computation | async-start | bytes 524288 | tf_op jit(solution)/shard_map/all_to_all | solution.py:294
  14.0 11.4 %copy-start.4 = (s32[1,1,3]{2,1,0:T(1,128)S(1)}, s32[1,1,3]{2,1,0:T(1,128)}, u32[]{:S(2)}) copy-start(s32[1,1,3]{2,1,0:T(1,128)} %param.10) | copy-start | bytes 40
  14.0 18.1 %copy-start = (bf16[512,512]{1,0:T(8,128)(2,1)S(1)}, bf16[512,512]{1,0:T(8,128)(2,1)}, u32[]{:S(2)}) copy-start(bf16[512,512]{1,0:T(8,128)(2,1)} %constant.16.clone.left) | copy-start | bytes 1572868
  14.0 18.1 %copy-start.3 = (bf16[256,256]{1,0:T(8,128)(2,1)S(1)}, bf16[256,256]{1,0:T(8,128)(2,1)}, u32[]{:S(2)}) copy-start(bf16[256,256]{1,0:T(8,128)(2,1)} %constant.17.clone.right) | copy-start | bytes 393220
  14.2 17.9 %copy-start.2 = (f32[2,256,128]{2,1,0:T(8,128)S(1)}, f32[2,256,128]{2,1,0:T(8,128)}, u32[]{:S(2)}) copy-start(f32[2,256,128]{2,1,0:T(8,128)} %constant.18.clone.twist) | copy-start | bytes 786436
  17.9 14.2 %collective-permute-start.1 = (bf16[32,32,128]{2,1,0:T(8,128)(2,1)S(1)}, bf16[32,32,128]{2,1,0:T(8,128)(2,1)S(1)}, u32[]{:S(2)}, u32[]{:S(2)}) collective-permute-start(bf16[32,32,128]{2,1,0:T(8,128)(2,1)S(1)} %all-to-all-done.own), channel_id=1, source_target_pairs={{0,16},{16,0},{1,17},{17,1},{2,18},{18,2},{3,19},{19,3},{4,20},{20... | collective-permute-start | bytes 786440 | tf_op jit(solution)/shard_map/ppermute | solution.py:301
  25.5 5.8 %collective-permute-start = (s32[1,5]{1,0:T(1,128)S(1)}, s32[1,5]{1,0:T(1,128)S(1)}, u32[]{:S(2)}, u32[]{:S(2)}) collective-permute-start(s32[1,5]{1,0:T(1,128)S(1)} %pad_add_fusion.mine), channel_id=1, source_target_pairs={{0,8},{8,0},{1,9},{9,1},{2,10},{10,2},{3,11},{11,3},{4,12},{12,4},... | collective-permute-start | bytes 68 | tf_op jit(solution)/shard_map/ppermute | solution.py:298

commit v9 on v8

--- a/solution.py
+++ b/solution.py
@@ -20,8 +20,8 @@
 FIELD_ROWS = 32 * OWN
 EXTRA = 8
 PEERS = 32
-PLANE_FIRST = 20
-SUM_FIRST = 12
+PLANE_FIRST = 21
+SUM_FIRST = 14
 PAIRS = [(0, 0, 0), (1, 1, 0), (0, 1, 0), (0, 1, 1), (2, 0, 0), (2, 0, 1), (3, 1, 0), (3, 1, 1)]
 
 
@@ -90,10 +90,10 @@
     for source, parity in ((own, core[0, 0]), (other, 1 - core[0, 0])):
         for q in range(2):
             for j in range(OCC):
-                for m in range(0, 16, 4):
+                for m in range(16):
                     at = (16 * q + m) ^ PLANE_FIRST
-                    planes = source[at : at + 4, 16 * j : 16 * j + 16].astype(jnp.float32)
-                    rows[q, j, m : m + 4, pl.ds(parity, 1)] = planes[:, None]
+                    planes = source[at : at + 1, 16 * j : 16 * j + 16].astype(jnp.float32)
+                    rows[q, j, m : m + 1, pl.ds(parity, 1)] = planes[:, None]
     for q in range(2):
         for j in range(OCC):
             for part in range(2):
@@ -162,9 +162,9 @@
         for part, value in enumerate((re, im)):
             value = value.astype(jnp.bfloat16).reshape(16, 16, 128)
             first = 32 * band + 16 * part
-            for to in range(0, 16, 4):
+            for to in range(16):
                 at = to ^ SUM_FIRST
-                out[at : at + 4, first : first + 16] = value[to : to + 4]
+                out[at : at + 1, first : first + 16] = value[to : to + 1]
         for slot, place, cross in PAIRS:
             if place == band:
                 if cross:

time: 56.6 us -> 57 us (level)
  waiting for transfers between devices: 4.67 us -> 6.56 us
  starting transfers between devices: 24.1 us -> 22.5 us
    all_to_all x1, waiting for transfers between devices: 3.61 us -> 5.09 us  [local(): lax.all_to_all(operand, ('xh', 'chip'), 0, 0, axis_index_groups=order(PEE...]
    all_to_all x1, starting transfers between devices: 12.5 us -> 11.7 us  [local(): lax.all_to_all(operand, ('xh', 'chip'), 0, 0, axis_index_groups=order(PEE...]
where the time goes in v9:
time: 57 us; the launch traced here: 56.7 us
  starting transfers between devices  22.5 us (39%)
  blocking collectives  20.9 us (37%)
  waiting for transfers between devices  6.56 us (12%)
  Pallas kernels  4.27 us (7%)
  local copies, waits for them, and re-layouts  1.54 us (3%)
  between operations  0.78 us (1%)
    all_to_all x1, blocking collectives, local(): lax.all_to_all(shares, ('xh', 'zz'), 0, 0, axis_index_groups=order(16, SU...  20.9 us
    all_to_all x1, starting transfers between devices, local(): lax.all_to_all(operand, ('xh', 'chip'), 0, 0, axis_index_groups=order(PEE...  11.7 us
    ppermute x1, starting transfers between devices, local(): swapped = lax.ppermute(gathered, 'core', [(0, 1), (1, 0)])  6.51 us
    all_to_all x1, waiting for transfers between devices, local(): lax.all_to_all(operand, ('xh', 'chip'), 0, 0, axis_index_groups=order(PEE...  5.09 us
    ppermute x1, starting transfers between devices, local(): theirs = lax.ppermute(mine, 'xh', [(0, 1), (1, 0)])  4.32 us
    pallas_call x4, Pallas kernels, call(): pl.pallas_call(kernel, out_shape=shapes, in_specs=specs, out_specs=jax.tr...  4.27 us
    ppermute x1, waiting for transfers between devices, local(): theirs = lax.ppermute(mine, 'xh', [(0, 1), (1, 0)])  1.47 us
  transfers between devices with their start and end apart: 3, of which 2 were waited for; matrix products, arithmetic and copies ran while one was open for 0% of the time, Pallas kernels for 2%

profile of v9, /device:TPU:1, one launch (start us, length us, event | category | flops | bytes accessed | tf_op | source)
XLA Modules:
  0.0 56.7 jit_solution(11802185400469785159)
XLA Ops:
  0.0 0.0 copy-start.1
  0.0 0.8 %reshape_squeeze.6 = bf16[2,2,8,128]{3,2,1,0:T(8,128)(2,1)S(1)} reshape(bf16[1,2,2,1024]{3,2,1,0:T(2,128)(2,1)} %param.8) | data formatting | bytes 16384 | tf_op jit(solution)/shard_map/reshape;squeeze | solution.py:285
  0.8 0.7 %broadcast_in_dim.8 = bf16[32,32,128]{2,1,0:T(8,128)(2,1)} broadcast(bf16[32,128]{1,0:T(8,128)(2,1)S(1)} %bitcast.16), dimensions={1,2} | broadcast | bytes 270336 | tf_op jit(solution)/shard_map/broadcast_in_dim | solution.py:293
  1.5 11.7 %all-to-all-start = ((bf16[32,32,128]{2,1,0:T(8,128)(2,1)}), bf16[32,32,128]{2,1,0:T(8,128)(2,1)S(1)}, u32[]{:S(2)}, u32[]{:S(2)}) async-start(bf16[32,32,128]{2,1,0:T(8,128)(2,1)} %broadcast_in_dim.8), calls=%async_computation | async-start | bytes 524288 | tf_op jit(solution)/shard_map/all_to_all | solution.py:294
  13.2 0.0 copy-done.1
  13.2 0.0 copy-start.4
  13.2 0.0 copy-start
  13.3 0.0 copy-start.3
  13.3 0.2 shard_map.74.targets
  13.5 0.0 copy-start.2
  13.5 5.1 %all-to-all-done.own = bf16[32,32,128]{2,1,0:T(8,128)(2,1)S(1)} async-done(((bf16[32,32,128]{2,1,0:T(8,128)(2,1)}), bf16[32,32,128]{2,1,0:T(8,128)(2,1)S(1)}, u32[]{:S(2)}, u32[]{:S(2)}) %all-to-all-start) | async-done | bytes 262176 | tf_op jit(solution)/shard_map/all_to_all | solution.py:294
  18.6 6.5 %collective-permute-start.1 = (bf16[32,32,128]{2,1,0:T(8,128)(2,1)S(1)}, bf16[32,32,128]{2,1,0:T(8,128)(2,1)S(1)}, u32[]{:S(2)}, u32[]{:S(2)}) collective-permute-start(bf16[32,32,128]{2,1,0:T(8,128)(2,1)S(1)} %all-to-all-done.own), channel_id=1, source_target_pairs={{0,16},{16,0},{1,17},{17,1},{2,18},{18,2},{3,19},{19,3},{4,20},{20... | collective-permute-start | bytes 786440 | tf_op jit(solution)/shard_map/ppermute | solution.py:301
  25.7 0.0 copy-done.4
  25.7 0.1 pad_add_fusion.mine
  25.8 4.3 %collective-permute-start = (s32[1,5]{1,0:T(1,128)S(1)}, s32[1,5]{1,0:T(1,128)S(1)}, u32[]{:S(2)}, u32[]{:S(2)}) collective-permute-start(s32[1,5]{1,0:T(1,128)S(1)} %pad_add_fusion.mine), channel_id=1, source_target_pairs={{0,8},{8,0},{1,9},{9,1},{2,10},{10,2},{3,11},{11,3},{4,12},{12,4},... | collective-permute-start | bytes 68 | tf_op jit(solution)/shard_map/ppermute | solution.py:298
  30.1 1.5 %collective-permute-done.theirs = s32[1,5]{1,0:T(1,128)S(1)} collective-permute-done((s32[1,5]{1,0:T(1,128)S(1)}, s32[1,5]{1,0:T(1,128)S(1)}, u32[]{:S(2)}, u32[]{:S(2)}) %collective-permute-start) | collective-permute-done | bytes 52 | tf_op jit(solution)/shard_map/ppermute | solution.py:298
  31.6 0.8 %shard_map.73.kernel = f32[2,256,128]{2,1,0:T(8,128)S(1)} custom-call(s32[1,5]{1,0:T(1,128)S(1)} %pad_add_fusion.mine, s32[1,5]{1,0:T(1,128)S(1)} %collective-permute-done.theirs), custom_call_target="tpu_custom_call" | custom-call | tf_op jit(solution)/shard_map/pallas_call | solution.py:246
  32.4 0.0 collective-permute-done.1.other
  32.4 0.0 copy-done
  32.4 0.0 copy-done.3
  32.4 0.0 copy-done.2
  32.4 2.5 %shard_map.75 = bf16[16,72,128]{2,1,0:T(8,128)(2,1)S(1)} custom-call(s32[1,1]{1,0:T(1,128)} %bitcast.core, f32[2,256,128]{2,1,0:T(8,128)S(1)} %shard_map.73.kernel, f32[4,2,256,128]{3,2,1,0:T(8,128)S(1)} %shard_map.74.targets, bf16[32,32,128]{2,1,0:T(8,128)(2,1)S(1)} %all-to-all-done.own, bf16[32,32,128]{2,1,0:T(8,128)(2,1)S(1)} %collective-permute-done.1.other, ...), custom_call_target="tpu_custom_call" | custom-call | tf_op jit(solution)/shard_map/pallas_call | solution.py:246
  34.9 20.9 %all_to_all.10.shares = bf16[16,72,128]{2,1,0:T(8,128)(2,1)S(1)} all-to-all(bf16[16,72,128]{2,1,0:T(8,128)(2,1)S(1)} %shard_map.75), channel_id=1, replica_groups={{14,15,12,13,10,11,8,9,6,7,4,5,2,3,0,1},{30,31,28,29,26,27,24,25,22,23,..., dimensions={0} | all-to-all | bytes 589824 | tf_op jit(solution)/shard_map/all_to_all | solution.py:304
  55.8 0.9 %shard_map.76 = f32[256,128]{1,0:T(8,128)} custom-call(bf16[16,72,128]{2,1,0:T(8,128)(2,1)S(1)} %all_to_all.10.shares), custom_call_target="tpu_custom_call" | custom-call | tf_op jit(solution)/shard_map/pallas_call | solution.py:246
  (1 shorter events, 0.0 us)
Async XLA Ops:
  0.0 13.2 %copy-start.1 = (bf16[1,4,2,32768]{3,2,1,0:T(2,128)(2,1)S(1)}, bf16[1,4,2,32768]{3,2,1,0:T(2,128)(2,1)}, u32[]{:S(2)}) copy-start(bf16[1,4,2,32768]{3,2,1,0:T(2,128)(2,1)} %param.7) | copy-start | bytes 1572868
  1.5 17.0 %all-to-all-start = ((bf16[32,32,128]{2,1,0:T(8,128)(2,1)}), bf16[32,32,128]{2,1,0:T(8,128)(2,1)S(1)}, u32[]{:S(2)}, u32[]{:S(2)}) async-start(bf16[32,32,128]{2,1,0:T(8,128)(2,1)} %broadcast_in_dim.8), calls=%async_computation | async-start | bytes 524288 | tf_op jit(solution)/shard_map/all_to_all | solution.py:294
  13.2 12.5 %copy-start.4 = (s32[1,1,3]{2,1,0:T(1,128)S(1)}, s32[1,1,3]{2,1,0:T(1,128)}, u32[]{:S(2)}) copy-start(s32[1,1,3]{2,1,0:T(1,128)} %param.10) | copy-start | bytes 40
  13.2 19.1 %copy-start = (bf16[512,512]{1,0:T(8,128)(2,1)S(1)}, bf16[512,512]{1,0:T(8,128)(2,1)}, u32[]{:S(2)}) copy-start(bf16[512,512]{1,0:T(8,128)(2,1)} %constant.16.clone.left) | copy-start | bytes 1572868
  13.3 19.1 %copy-start.3 = (bf16[256,256]{1,0:T(8,128)(2,1)S(1)}, bf16[256,256]{1,0:T(8,128)(2,1)}, u32[]{:S(2)}) copy-start(bf16[256,256]{1,0:T(8,128)(2,1)} %constant.17.clone.right) | copy-start | bytes 393220
  13.5 19.0 %copy-start.2 = (f32[2,256,128]{2,1,0:T(8,128)S(1)}, f32[2,256,128]{2,1,0:T(8,128)}, u32[]{:S(2)}) copy-start(f32[2,256,128]{2,1,0:T(8,128)} %constant.18.clone.twist) | copy-start | bytes 786436
  18.6 13.8 %collective-permute-start.1 = (bf16[32,32,128]{2,1,0:T(8,128)(2,1)S(1)}, bf16[32,32,128]{2,1,0:T(8,128)(2,1)S(1)}, u32[]{:S(2)}, u32[]{:S(2)}) collective-permute-start(bf16[32,32,128]{2,1,0:T(8,128)(2,1)S(1)} %all-to-all-done.own), channel_id=1, source_target_pairs={{0,16},{16,0},{1,17},{17,1},{2,18},{18,2},{3,19},{19,3},{4,20},{20... | collective-permute-start | bytes 786440 | tf_op jit(solution)/shard_map/ppermute | solution.py:301
  25.8 5.8 %collective-permute-start = (s32[1,5]{1,0:T(1,128)S(1)}, s32[1,5]{1,0:T(1,128)S(1)}, u32[]{:S(2)}, u32[]{:S(2)}) collective-permute-start(s32[1,5]{1,0:T(1,128)S(1)} %pad_add_fusion.mine), channel_id=1, source_target_pairs={{0,8},{8,0},{1,9},{9,1},{2,10},{10,2},{3,11},{11,3},{4,12},{12,4},... | collective-permute-start | bytes 68 | tf_op jit(solution)/shard_map/ppermute | solution.py:298
